TPU v7x, 512 devices: a whole 4x8x8 slice. The times are simulated.
512 devices in a mesh: gx: 32 (over z_hi, x, core), gy: 16 (over z_lo, y).
Axes of the slice: x: 4, y: 8, z: 8 (z_hi: 4, z_lo: 2; z = z_hi * 2 + z_lo), core: 2. Of those that a mesh axis runs over, the one named last changes fastest.
Arguments:
- core_one: bfloat16 [200, 128], replicated, may hold values from -6 to 6
- core_two: bfloat16 [200, 4096], replicated, may hold values from -1 to 1
- core_three: bfloat16 [250, 256], replicated, may hold values from -1 to 1
- dense_rows: bfloat16 [32768, 128], P(('gx', 'gy')), may hold values from -24 to 24
- w_top: bfloat16 [256, 256], replicated, may hold values from -0.375 to 0.375
- bias_top: float32 [256], replicated, may hold values from -3 to 3
- w_out: float32 [256], replicated, may hold values from -0.75 to 0.75
- labels: int32 [32768], P(('gx', 'gy')), may hold values 0 or 1
- bag_ids: int32 [512, 256], P(('gx', 'gy')), may hold values from 0 to 63, never falling along the last dimension, each value on 1 to 8 neighbouring positions
- digit_one: int32 [512, 256], P(('gx', 'gy')), may hold values from 0 to 199
- digit_two: int32 [512, 256], P(('gx', 'gy')), may hold values from 0 to 199
- digit_three: int32 [512, 256], P(('gx', 'gy')), may hold values from 0 to 249
Outputs:
- core_grad: float32 [908800], P(('gx', 'gy'))
- top_grad: float32 [258, 256], replicated
Inputs may be any that keep to these rules, and one draw needn't show every extreme that they name: `bag_ids`: along a row, never falling; every sample of the block gets 1 to 8 lookups, one exactly 8.
All inputs are finite; a program needn't handle non-finite values. No bound on the sum of `labels` on one device may be relied on, other than what follows from the above.
Results may differ from a plain program's by a relative error of at most 0.0018.
The roundings to bfloat16 on the way count: a program that leaves them out, or rounds other values in their place, can miss the bound.
Values sent between devices are 32-bit elements; how exact they have to be, the bound alone decides.
A program may use at most 64 MiB of HBM per device.

v0:
```python
import jax
import jax.numpy as jnp
from jax import lax
from jax.sharding import PartitionSpec as P

D1 = 4
D2 = 4
D3 = 8
R = 32


def one_hot(digits, count, kind):
    return (digits[:, None] == jnp.arange(count, dtype=jnp.int32)[None, :]).astype(kind)


def slices(digits, core):
    return jnp.dot(
        one_hot(digits, core.shape[0], jnp.bfloat16), core, preferred_element_type=jnp.float32
    )


def factors(digits, cores):
    high = lax.Precision.HIGHEST
    first = slices(digits[0], cores[0]).reshape(-1, D1, R)
    middle = slices(digits[1], cores[1]).reshape(-1, R, D2 * R)
    last = slices(digits[2], cores[2]).reshape(-1, R, D3)
    left = jnp.einsum("nia,nab->nib", first, middle, precision=high).reshape(-1, D1 * D2, R)
    return (first, middle, last, left)


def top_total(top_local):
    return lax.psum(top_local, ("gx", "gy"))


def per_device(
    core_one,
    core_two,
    core_three,
    dense_rows,
    w_top,
    bias_top,
    w_out,
    labels,
    bag_ids,
    digit_one,
    digit_two,
    digit_three,
):
    high = lax.Precision.HIGHEST
    cores = (core_one, core_two, core_three)
    digits = jnp.stack([digit_one[0], digit_two[0], digit_three[0]])
    looks = digits.shape[1]
    block = min(256, looks)
    blocks = looks // block
    blocked = digits.reshape(3, blocks, block).transpose(1, 0, 2)
    width = D1 * D2 * D3

    def forward(carry, part):
        first, middle, last, left = factors(part, cores)
        return (carry, jnp.einsum("npa,nad->npd", left, last, precision=high).reshape(block, width))

    _, embedded = lax.scan(forward, jnp.zeros((), jnp.float32), blocked)
    embedded = embedded.reshape(looks, width)
    samples = dense_rows.shape[0]
    bag_table = one_hot(bag_ids[0], samples, jnp.float32)
    pooled = jnp.dot(bag_table.T, embedded, precision=high)
    joined = jnp.concatenate([dense_rows, pooled.astype(jnp.bfloat16)], axis=1)
    pre = jnp.dot(joined, w_top, preferred_element_type=jnp.float32) + bias_top[None, :]
    sig = jax.nn.sigmoid(pre)
    hidden = pre * sig
    logit = jnp.dot(hidden, w_out, precision=high)
    dlogit = (jax.nn.sigmoid(logit) - labels.astype(jnp.float32)) / samples
    dpre = dlogit[:, None] * w_out[None, :] * (sig * (1.0 + pre * (1.0 - sig)))
    dpre_low = dpre.astype(jnp.bfloat16)
    grad_weight = jnp.dot(joined.T, dpre_low, preferred_element_type=jnp.float32)
    grad_bias = jnp.sum(dpre, axis=0)
    grad_output = jnp.sum(hidden * dlogit[:, None], axis=0)
    top_local = jnp.concatenate([grad_weight, grad_bias[None, :], grad_output[None, :]], axis=0)
    grad_pooled = jnp.dot(dpre_low, w_top[width:].T, preferred_element_type=jnp.float32)
    grad_embedded = jnp.dot(bag_table, grad_pooled, precision=high).reshape(blocks, block, width)

    def backward(totals, inputs):
        part, grad_block = inputs
        first, middle, last, left = factors(part, cores)
        grad_view = grad_block.reshape(block, D1 * D2, D3)
        grad_last = jnp.einsum("npa,npd->nad", left, grad_view, precision=high)
        grad_left = jnp.einsum("npd,nad->npa", grad_view, last, precision=high).reshape(
            block, D1, D2 * R
        )
        grad_first = jnp.einsum("nib,nab->nia", grad_left, middle, precision=high)
        grad_middle = jnp.einsum("nia,nib->nab", first, grad_left, precision=high)
        pieces = (
            grad_first.reshape(block, -1),
            grad_middle.reshape(block, -1),
            grad_last.reshape(block, -1),
        )
        updated = tuple(
            (
                total
                + jnp.dot(
                    one_hot(part[number], cores[number].shape[0], jnp.float32).T,
                    pieces[number],
                    precision=high,
                )
                for number, total in enumerate(totals)
            )
        )
        return (updated, None)

    start = tuple((jnp.zeros(core.shape, jnp.float32) for core in cores))
    totals, _ = lax.scan(backward, start, (blocked, grad_embedded))
    flat = jnp.concatenate([total.reshape(-1) for total in totals])
    core_grad = lax.psum_scatter(flat, ("gx", "gy"), scatter_dimension=0, tiled=True)
    top_grad = top_total(top_local)
    return (core_grad, top_grad)


def solution(mesh):
    return jax.shard_map(
        per_device,
        mesh=mesh,
        in_specs=(
            P(),
            P(),
            P(),
            P(("gx", "gy"), None),
            P(),
            P(),
            P(),
            P(("gx", "gy")),
            P(("gx", "gy"), None),
            P(("gx", "gy"), None),
            P(("gx", "gy"), None),
            P(("gx", "gy"), None),
        ),
        out_specs=(P(("gx", "gy")), P()),
        check_vma=False,
    )
```

profile of v0, /device:TPU:1, one launch (start us, length us, event | category | flops | bytes accessed | tf_op | source)
XLA Modules:
  0.0 379.1 jit_solution(1021754452984947025)
XLA Ops:
  7.2 1.2 fusion.16
  8.4 0.2 copy.35
  8.7 1.2 convolution_bitcast_fusion.2
  9.9 0.4 copy.38
  10.4 1.4 convolution_bitcast_fusion.1
  11.8 0.8 copy.50
  12.6 1.9 copy-done.1
  14.5 4.2 %fusion.41 = f32[256,4,128]{2,1,0:T(4,128)} fusion(f32[256,4,32]{2,1,0:T(4,128)S(1)} %copy.35, f32[256,32,128]{2,1,0:T(8,128)S(1)} %bitcast.68), kind=kOutput, calls=%fused_computation.52 | convolution fusion | flops 50331648 | bytes 4849664 | tf_op jit(solution)/shard_map/while/body/eval_jaxpr/nia,nab->nib/dot_general | solution.py:27
  18.8 2.1 copy.36
  20.8 3.6 copy.37
  24.5 6.0 %fusion.42 = f32[256,16,8]{1,2,0:T(8,128)} fusion(f32[256,16,32]{2,1,0:T(8,128)} %copy.37, f32[256,32,8]{1,2,0:T(8,128)S(1)} %copy.38), kind=kOutput, calls=%fused_computation.53 | convolution fusion | flops 12582912 | bytes 917504 | tf_op jit(solution)/shard_map/while/body/eval_jaxpr/npa,nad->npd/dot_general | solution.py:60
  30.4 1.5 copy.39
  32.0 0.3 convolution_convert_fusion
  33.0 0.9 fusion.33
  33.9 0.3 convolution_bitcast_fusion.3
  34.2 1.4 copy.40
  35.6 5.1 %fusion.46 = f32[256,32,8]{1,2,0:T(8,128)} fusion(f32[256,16,32]{2,1,0:T(8,128)} %copy.37, f32[256,16,8]{1,2,0:T(8,128)} %copy.40), kind=kOutput, calls=%fused_computation.57 | convolution fusion | flops 12582912 | bytes 917504 | tf_op jit(solution)/shard_map/while/body/eval_jaxpr/npa,npd->nad/dot_general | solution.py:86
  40.8 4.8 %fusion.43 = f32[256,16,32]{2,1,0:T(8,128)} fusion(f32[256,16,8]{1,2,0:T(8,128)S(1)} %copy-done.2, f32[256,32,8]{1,2,0:T(8,128)S(1)} %copy.38), kind=kOutput, calls=%fused_computation.54 | convolution fusion | flops 12582912 | bytes 917504 | tf_op jit(solution)/shard_map/while/body/eval_jaxpr/npd,nad->npa/dot_general | solution.py:87
  45.6 2.5 copy.42
  48.3 8.3 %fusion.44 = f32[256,4,32]{2,1,0:T(4,128)S(1)} fusion(f32[256,4,128]{2,1,0:T(4,128)S(1)} %copy.43, f32[256,32,128]{2,1,0:T(8,128)} %bitcast.69), kind=kOutput, calls=%fused_computation.55 | convolution fusion | flops 50331648 | bytes 4849664 | tf_op jit(solution)/shard_map/while/body/eval_jaxpr/nib,nab->nia/dot_general | solution.py:90
  56.6 8.3 %fusion.45 = f32[256,32,128]{2,1,0:T(8,128)} fusion(f32[256,4,32]{2,1,0:T(4,128)S(1)} %copy.35, f32[256,4,128]{2,1,0:T(4,128)S(1)} %copy.43), kind=kOutput, calls=%fused_computation.56 | convolution fusion | flops 50331648 | bytes 4849664 | tf_op jit(solution)/shard_map/while/body/eval_jaxpr/nia,nib->nab/dot_general | solution.py:91
  64.9 1.6 copy.49
  66.5 0.4 fusion.12
  67.1 0.3 convolution_bitcast_fusion
  67.5 6.6 %fusion.3 = f32[25,32,8,128]{3,2,1,0:T(8,128)S(1)} fusion(f32[32,8,32,128]{3,2,1,0:T(8,128)} %bitcast.70, s32[256]{0:T(256)S(1)} %bitcast.77), kind=kOutput, calls=%fused_computation.6 | convolution fusion | flops 2516633600 | bytes 7472128 | tf_op jit(solution)/shard_map/while/body/eval_jaxpr/dot_general | solution.py:100
  74.1 0.6 copy.52
  74.7 0.4 copy-done.3
  75.0 0.7 pad_maximum_fusion.1
  75.8 2.1 pad_maximum_fusion
  77.9 291.3 %all-reduce.4.cloned.1.call-done = (f32[908800]{0:T(1024)}, f32[258,256]{1,0:T(8,128)}) async-done(((f32[908800]{0:T(1024)}, f32[258,256]{1,0:T(8,128)}), (f32[908800]{0:T(1024)}, f32[258,256]{1,0:T(8,128)})) %all-reduce.4.cloned.1.call-update) | async-done | bytes 3899408
  369.2 1.4 dynamic-slice.2
  370.6 1.7 copy.61
  (33 shorter events, 1.2 us)
Async XLA Ops:
  7.2 3.2 copy-start
  7.2 362.0 %all-reduce.4.cloned.1.call-start = ((), (), s32[]{:S(2)}) async-start(), calls=%async_computation | async-start | bytes 7815168
  12.6 1.9 copy-start.1
  20.8 11.1 %copy-start.7 = (s32[1,256]{1,0:T(1,128)S(1)}, s32[1,256]{1,0:T(1,128)}, u32[]{:S(2)}) copy-start(s32[1,256]{1,0:T(1,128)} %param.20) | copy-start | bytes 3076
  20.8 11.5 %copy-start.4 = (bf16[256,256]{1,0:T(8,128)(2,1)S(1)}, bf16[256,256]{1,0:T(8,128)(2,1)}, u32[]{:S(2)}) copy-start(bf16[256,256]{1,0:T(8,128)(2,1)} %param.16) | copy-start | bytes 393220
  20.8 11.5 %copy-start.6 = (bf16[64,128]{1,0:T(8,128)(2,1)S(1)}, bf16[64,128]{1,0:T(8,128)(2,1)}, u32[]{:S(2)}) copy-start(bf16[64,128]{1,0:T(8,128)(2,1)} %param.15) | copy-start | bytes 49156
  20.8 11.5 %copy-start.10 = (f32[256]{0:T(256)S(1)}, f32[256]{0:T(256)}, u32[]{:S(2)}) copy-start(f32[256]{0:T(256)} %param.17) | copy-start | bytes 3076
  20.8 11.6 %copy-start.11 = (f32[256]{0:T(256)S(1)}, f32[256]{0:T(256)}, u32[]{:S(2)}) copy-start(f32[256]{0:T(256)} %param.18) | copy-start | bytes 3076
  20.8 11.6 %copy-start.12 = (s32[64]{0:T(128)S(1)}, s32[64]{0:T(128)}, u32[]{:S(2)}) copy-start(s32[64]{0:T(128)} %param.19) | copy-start | bytes 772
  35.6 5.1 %copy-start.2 = (f32[256,16,8]{1,2,0:T(8,128)S(1)}, f32[256,16,8]{1,2,0:T(8,128)}, u32[]{:S(2)}) copy-start(f32[256,16,8]{1,2,0:T(8,128)} %copy.40) | copy-start | bytes 393220
  56.6 9.9 %copy-start.8 = (s32[1,256]{1,0:T(1,128)S(1)}, s32[1,256]{1,0:T(1,128)}, u32[]{:S(2)}) copy-start(s32[1,256]{1,0:T(1,128)} %param.23) | copy-start | bytes 3076
  56.6 10.5 %copy-start.9 = (s32[1,256]{1,0:T(1,128)S(1)}, s32[1,256]{1,0:T(1,128)}, u32[]{:S(2)}) copy-start(s32[1,256]{1,0:T(1,128)} %param.21) | copy-start | bytes 3076
  56.6 10.8 %copy-start.5 = (s32[1,256]{1,0:T(1,128)S(1)}, s32[1,256]{1,0:T(1,128)}, u32[]{:S(2)}) copy-start(s32[1,256]{1,0:T(1,128)} %param.22) | copy-start | bytes 3076
  74.1 1.0 copy-start.3
Sparse Core Ops, SparseCore 0:
  78.0 291.1 all-reduce.3
where the time goes:
time: 380 us; the launch traced here: 379 us
  waiting for transfers between devices  291 us (77%)
  matrix products  50 us (13%)
  local copies, waits for them, and re-layouts  20.5 us (5%)
  between operations  14.3 us (4%)
    unnamed x2, waiting for transfers between devices  291 us
    dot_general x1, matrix products, backward(): grad_first = jnp.einsum('nib,nab->nia', grad_left, middle, precision=high)  8.32 us
    dot_general x1, matrix products, backward(): grad_middle = jnp.einsum('nia,nib->nab', first, grad_left, precision=high)  8.26 us
  transfers between devices with their start and end apart: 1, of which 1 were waited for; matrix products, arithmetic and copies ran while one was open for 0% of the time, Pallas kernels for 0%

commit v1 on v0

--- a/solution.py
+++ b/solution.py
@@ -1,6 +1,10 @@
+import functools
+
 import jax
 import jax.numpy as jnp
 from jax import lax
+from jax.experimental import pallas as pl
+from jax.experimental.pallas import tpu as pltpu
 from jax.sharding import PartitionSpec as P
 
 D1 = 4
@@ -28,8 +32,227 @@
     return (first, middle, last, left)
 
 
-def top_total(top_local):
-    return lax.psum(top_local, ("gx", "gy"))
+MESH = pl.DeviceIdType.MESH
+ORDER = (1, 7, 2, 6, 3, 5, 4)
+XORDER = (1, 3, 2)
+
+
+def whereabouts():
+    gx, gy = lax.axis_index("gx"), lax.axis_index("gy")
+    core, x = gx % 2, (gx // 2) % 4
+    y, z = gy % 8, (gx // 8) * 2 + gy // 8
+    u = (1 - core) * y + core * z
+    v = (1 - core) * z + core * y
+    return core, x, u, v
+
+
+def place(core, x, u, v):
+    y = (1 - core) * u + core * v
+    z = core * u + (1 - core) * v
+    return ((z // 2) * 8 + x * 2 + core, (z % 2) * 8 + y)
+
+
+def summed(rows, step, store, *parts):
+    def body(i, carry):
+        at = pl.ds(pl.multiple_of(i * step, step), step)
+        total = parts[0](at)
+        for part in parts[1:]:
+            total = total + part(at)
+        store(at, total)
+        return carry
+
+    lax.fori_loop(0, rows // step, body, 0)
+
+
+def exchange_kernel(w, t, e, out, top, r0, s1, r1a, r1b, s2a, s2b, r2a, r2b, s3a, s3b, r3a, r3b,
+                    rt0, re0, st1, rt1, st2, rt2, rt3, g1, g2, g3, send, recv):
+    core, x, u, v = whereabouts()
+    y = (1 - core) * u + core * v
+    z = core * u + (1 - core) * v
+    mate = ((z // 2) * 8 + x * 2 + (1 - core), (z % 2) * 8 + y)
+    other_x = {k: place(core, (x + k) % 4, u, v) for k in XORDER}
+    other_u = {k: place(core, x, (u + k) % 8, v) for k in ORDER}
+    other_v = {k: place(core, x, u, (v + k) % 8) for k in ORDER}
+    barrier = pltpu.get_barrier_semaphore()
+    peers = [mate] + list(other_x.values()) + list(other_u.values()) + list(other_v.values())
+    for peer in peers:
+        pl.semaphore_signal(barrier, inc=1, device_id=peer, device_id_type=MESH)
+    pl.semaphore_wait(barrier, len(peers))
+    copies = []
+
+    def put(src, dst, peer):
+        spot = len(copies)
+        copy = pltpu.make_async_remote_copy(
+            src_ref=src, dst_ref=dst, send_sem=send.at[spot], recv_sem=recv.at[spot],
+            device_id=peer, device_id_type=MESH)
+        copy.start()
+        copies.append(copy)
+        return copy
+
+    def arrived(group):
+        for copy in group:
+            copy.wait_recv()
+
+    t0 = [put(t.at[1 - core], rt0, mate), put(e, re0, mate)]
+    p0 = [put(w.at[1 - core, color], r0.at[color], mate) for color in (0, 1)]
+    arrived(t0)
+    extra = e[...] + re0[...]
+    for part in range(4):
+        rows = pl.ds(part * 64, 64)
+        st1[part, 0:64, :] = t[core, rows, :] + rt0[rows, :]
+        st1[part, 64:72, :] = extra
+    t1 = [put(st1.at[(x + k) % 4], rt1.at[x], other_x[k]) for k in XORDER]
+    rt1[x] = st1[x]
+
+    def fold(color):
+        def store(at, value):
+            s1[color, at, :] = value
+        summed(2048, 256, store, lambda at: w[core, color, at, :], lambda at: r0[color, at, :])
+
+    arrived(p0[:1])
+    fold(0)
+    p1a = [put(s1.at[0, pl.ds(((x + k) % 4) * 512, 512)], r1a.at[k - 1], other_x[k]) for k in XORDER]
+    arrived(p0[1:])
+    fold(1)
+    p1b = [put(s1.at[1, pl.ds(((u + k) % 8) * 256, 256)], r1b.at[k - 1], other_u[k]) for k in ORDER]
+
+    arrived(t1)
+    total = rt1[0]
+    for part in range(1, 4):
+        total = total + rt1[part]
+    for part in range(8):
+        st2[part, 0:8, :] = total[part * 8:part * 8 + 8]
+        st2[part, 8:16, :] = total[64:72]
+    t2 = [put(st2.at[(v + k) % 8], rt2.at[v], other_v[k]) for k in ORDER]
+    rt2[v] = st2[v]
+    arrived(t2)
+    total = rt2[0]
+    for part in range(1, 8):
+        total = total + rt2[part]
+    rt3[u] = total
+    t3 = [put(rt3.at[u], rt3.at[u], other_u[k]) for k in ORDER]
+
+    arrived(p1a)
+
+    def store2a(at, value):
+        s2a[at, :] = value
+
+    summed(512, 128, store2a, lambda at: s1[0, pl.ds(x * 512 + at.start, at.size), :],
+           *[functools.partial(lambda k, at: r1a[k, at, :], k) for k in range(3)])
+    p2a = [put(s2a.at[pl.ds(((u + k) % 8) * 64, 64)], r2a.at[k - 1], other_u[k]) for k in ORDER]
+    arrived(p1b)
+
+    def store2b(at, value):
+        s2b[at, :] = value
+
+    summed(256, 64, store2b, lambda at: s1[1, pl.ds(u * 256 + at.start, at.size), :],
+           *[functools.partial(lambda k, at: r1b[k, at, :], k) for k in range(7)])
+    p2b = [put(s2b.at[pl.ds(((v + k) % 8) * 32, 32)], r2b.at[k - 1], other_v[k]) for k in ORDER]
+
+    arrived(t3)
+    total = rt3[0]
+    for part in range(1, 8):
+        total = total + rt3[part]
+    g1[v] = total[0:8]
+    extra = total[8:16]
+    t4 = [put(g1.at[v], g1.at[v], other_v[k]) for k in ORDER]
+
+    arrived(p2a)
+    total = s2a[pl.ds(u * 64, 64), :]
+    for part in range(7):
+        total = total + r2a[part]
+    s3a[...] = total
+    p3a = [put(s3a.at[pl.ds(((v + k) % 8) * 8, 8)], r3a.at[k - 1], other_v[k]) for k in ORDER]
+    arrived(p2b)
+    total = s2b[pl.ds(v * 32, 32), :]
+    for part in range(7):
+        total = total + r2b[part]
+    s3b[...] = total
+    p3b = [put(s3b.at[pl.ds(((x + k) % 4) * 8, 8)], r3b.at[k - 1], other_x[k]) for k in XORDER]
+
+    arrived(t4)
+    g2[x] = g1[...]
+    t5 = [put(g2.at[x], g2.at[x], other_x[k]) for k in XORDER]
+    for copy in t5:
+        copy.wait_recv()
+    t6 = put(g2, g3, mate)
+
+    arrived(p3a)
+    upper = s3a[pl.ds(v * 8, 8), :]
+    for part in range(7):
+        upper = upper + r3a[part]
+    arrived(p3b)
+    lower = s3b[pl.ds(x * 8, 8), :]
+    for part in range(3):
+        lower = lower + r3b[part]
+    gx, gy = lax.axis_index("gx"), lax.axis_index("gy")
+    offset = ((gx * 16 + gy) * 1775) % 128
+    turned = pltpu.roll(jnp.concatenate([upper, lower], axis=0), (128 - offset) % 128, 1)
+    below = pltpu.roll(turned, 15, 0)
+    lane = lax.broadcasted_iota(jnp.int32, (16, 128), 1)
+    out[...] = jnp.where(lane < 128 - offset, turned, below)
+
+    top[256:257, 0:128] = extra[0:1]
+    top[256:257, 128:256] = extra[1:2]
+    top[257:258, 0:128] = extra[2:3]
+    top[257:258, 128:256] = extra[3:4]
+    arrived([t6])
+
+    @pl.when(core == 0)
+    def _():
+        top[0:256, 0:128] = g2[...].reshape(256, 128)
+        top[0:256, 128:256] = g3[...].reshape(256, 128)
+
+    @pl.when(core == 1)
+    def _():
+        top[0:256, 128:256] = g2[...].reshape(256, 128)
+        top[0:256, 0:128] = g3[...].reshape(256, 128)
+
+    for copy in copies:
+        copy.wait_send()
+
+
+def exchange(w, t, e):
+    f32 = jnp.float32
+    shapes = [(2, 2048), (2, 2048), (3, 512), (7, 256), (512,), (256,), (7, 64), (7, 32), (64,), (32,), (7, 8), (3, 8),
+              (256,), (8,), (4, 72), (4, 72), (8, 16), (8, 16), (8, 16), (8, 8), (4, 8, 8), (4, 8, 8)]
+    vmem = pl.BlockSpec(memory_space=pltpu.VMEM)
+    return pl.pallas_call(
+        exchange_kernel,
+        out_shape=(jax.ShapeDtypeStruct((16, 128), f32), jax.ShapeDtypeStruct((258, 256), f32)),
+        in_specs=[vmem] * 3,
+        out_specs=(vmem, vmem),
+        scratch_shapes=[pltpu.VMEM(shape + (128,), f32) for shape in shapes]
+        + [pltpu.SemaphoreType.DMA((70,)), pltpu.SemaphoreType.DMA((70,))],
+        compiler_params=pltpu.CompilerParams(collective_id=0, has_side_effects=True, vmem_limit_bytes=40 * 1024 * 1024),
+        name="exchange",
+    )(w, t, e)
+
+
+def pack_kernel(flat, w):
+    def body(q, carry):
+        b, x, y = (q // 16) % 2, (q // 32) % 4, q % 8
+        z = (q // 128) * 2 + (q // 8) % 2
+        u = (1 - b) * y + b * z
+        v = (1 - b) * z + b * y
+        rows = flat[pl.ds((1775 * q) // 128, 16), :]
+        w[b, 0, pl.ds(pl.multiple_of((x * 64 + u * 8 + v) * 8, 8), 8), :] = rows[0:8]
+        w[b, 1, pl.ds(pl.multiple_of((u * 32 + v * 4 + x) * 8, 8), 8), :] = rows[8:16]
+        return carry
+
+    lax.fori_loop(0, 512, body, 0)
+
+
+def pack(flat):
+    vmem = pl.BlockSpec(memory_space=pltpu.VMEM)
+    return pl.pallas_call(
+        pack_kernel,
+        out_shape=jax.ShapeDtypeStruct((2, 2, 2048, 128), jnp.float32),
+        in_specs=[vmem],
+        out_specs=vmem,
+        compiler_params=pltpu.CompilerParams(vmem_limit_bytes=20 * 1024 * 1024),
+        name="pack",
+    )(flat)
 
 
 def per_device(
@@ -110,9 +333,11 @@
     start = tuple((jnp.zeros(core.shape, jnp.float32) for core in cores))
     totals, _ = lax.scan(backward, start, (blocked, grad_embedded))
     flat = jnp.concatenate([total.reshape(-1) for total in totals])
-    core_grad = lax.psum_scatter(flat, ("gx", "gy"), scatter_dimension=0, tiled=True)
-    top_grad = top_total(top_local)
-    return (core_grad, top_grad)
+    packed = pack(jnp.pad(flat, (0, 512)).reshape(7104, 128))
+    sides = jnp.stack([top_local[:256, :128], top_local[:256, 128:]])
+    extra = jnp.pad(top_local[256:].reshape(4, 128), ((0, 4), (0, 0)))
+    chunk, top_grad = exchange(packed, sides, extra)
+    return (chunk.reshape(-1)[:1775], top_grad)
 
 
 def solution(mesh):

time: 380 us -> 142 us (0.37)
  waiting for transfers between devices: 291 us -> 0 us
  Pallas kernels: 0 us -> 66.6 us
  between operations: 14.3 us -> 0.91 us
    unnamed x2 -> x0, waiting for transfers between devices: 291 us -> none
    pallas_call x0 -> x2, Pallas kernels: none -> 66.6 us  [the longest x1 48.6 us: exchange(): pl.pallas_call(exchange_kernel, out_shape=(jax.ShapeDtypeStruct((16, 128)...]
  transfers between devices with their start and end apart: 1 -> 0, of which waited for: 1 -> 0; matrix products, arithmetic and copies ran while one was open for 0% -> 0% of each run, Pallas kernels for 0% -> 0%
where the time goes in v1:
time: 142 us; the launch traced here: 141 us
  Pallas kernels  66.6 us (47%)
  matrix products  50.4 us (35%)
  local copies, waits for them, and re-layouts  22.6 us (16%)
    pallas_call x1, Pallas kernels, exchange(): pl.pallas_call(exchange_kernel, out_shape=(jax.ShapeDtypeStruct((16, 128)...  48.6 us
    pallas_call x1, Pallas kernels, pack(): pl.pallas_call(pack_kernel, out_shape=jax.ShapeDtypeStruct((2, 2, 2048, 1...  18.1 us
    dot_general x1, matrix products, backward(): grad_first = jnp.einsum('nib,nab->nia', grad_left, middle, precision=high)  8.54 us
    dot_general x3, matrix products, backward(): jnp.dot(one_hot(part[number], cores[number].shape[0], jnp.float32).T, pie...  7.95 us
    dot_general x1, matrix products, backward(): grad_middle = jnp.einsum('nia,nib->nab', first, grad_left, precision=high)  6.74 us
    dot_general x1, matrix products, backward(): jnp.einsum('npd,nad->npa', grad_view, last, precision=high)  6.03 us
    dot_general x1, matrix products, forward(): jnp.einsum('npa,nad->npd', left, last, precision=high).reshape(block, width)  5.94 us
    dot_general x1, matrix products, backward(): grad_last = jnp.einsum('npa,npd->nad', left, grad_view, precision=high)  5.05 us

profile of v1, /device:TPU:1, one launch (start us, length us, event | category | flops | bytes accessed | tf_op | source)
XLA Modules:
  0.0 141.0 jit_solution(14786167494666652734)
XLA Ops:
  0.6 1.2 fusion.17
  1.9 1.2 convolution_bitcast_fusion.2
  3.3 0.4 copy.23
  3.8 1.4 %convolution_bitcast_fusion.1 = f32[32,8,32,128]{3,1,2,0:T(8,128)S(1)} fusion(bf16[200,4096]{1,0:T(8,128)(2,1)S(1)} %copy-done, s32[256]{0:T(256)} %bitcast.85), kind=kOutput, calls=%fused_computation.8 | convolution fusion | flops 419481600 | bytes 5833728 | tf_op jit(solution)/shard_map/while/body/eval_jaxpr/dot_general | solution.py:21
  5.2 0.8 copy.35
  6.0 1.9 %copy-done.1 = f32[32,8,32,128]{3,2,1,0:T(8,128)} copy-done((f32[32,8,32,128]{3,2,1,0:T(8,128)}, f32[32,8,32,128]{3,2,1,0:T(8,128)S(1)}, u32[]{:S(2)}) %copy-start.1) | copy-done | bytes 4194328
  7.9 4.2 %fusion.42 = f32[256,4,128]{2,1,0:T(4,128)} fusion(f32[256,4,32]{2,1,0:T(4,128)S(1)} %copy.20, f32[256,32,128]{2,1,0:T(8,128)S(1)} %bitcast.77), kind=kOutput, calls=%fused_computation.58 | convolution fusion | flops 50331648 | bytes 4849664 | tf_op jit(solution)/shard_map/while/body/eval_jaxpr/nia,nab->nib/dot_general | solution.py:31
  12.2 2.1 %copy.21 = f32[256,4,128]{0,2,1:T(8,128)} copy(f32[256,4,128]{2,1,0:T(4,128)} %fusion.42) | data formatting | bytes 1048576 | tf_op jit(solution)/shard_map/while/body/eval_jaxpr/nia,nab->nib/dot_general | solution.py:31
  14.3 3.6 %copy.22 = f32[256,16,32]{2,1,0:T(8,128)} copy(f32[256,16,32]{0,2,1:T(8,128)} %bitcast.81) | data formatting | bytes 1048576 | tf_op jit(solution)/shard_map/while/body/eval_jaxpr/reshape | solution.py:31
  17.9 5.9 %fusion.43 = f32[256,16,8]{1,2,0:T(8,128)} fusion(f32[256,16,32]{2,1,0:T(8,128)} %copy.22, f32[256,32,8]{1,2,0:T(8,128)S(1)} %copy.23), kind=kOutput, calls=%fused_computation.59 | convolution fusion | flops 12582912 | bytes 917504 | tf_op jit(solution)/shard_map/while/body/eval_jaxpr/npa,nad->npd/dot_general | solution.py:283
  23.8 1.5 %copy.24 = f32[256,16,8]{0,2,1:T(8,128)S(1)} copy(f32[256,16,8]{1,2,0:T(8,128)} %fusion.43) | data formatting | bytes 262144 | tf_op jit(solution)/shard_map/while/body/eval_jaxpr/npa,nad->npd/dot_general | solution.py:283
  25.4 0.3 convolution_convert_fusion
  26.4 1.0 convolution_bitcast_fusion.3
  27.7 2.2 %copy.25 = f32[256,16,8]{1,2,0:T(8,128)} copy(f32[256,16,8]{0,2,1:T(8,128)} %convolution_bitcast_fusion.3) | data formatting | bytes 262144 | tf_op jit(solution)/shard_map/while/body/eval_jaxpr/reshape | solution.py:308
  29.9 5.0 %fusion.47 = f32[256,32,8]{1,2,0:T(8,128)} fusion(f32[256,16,32]{2,1,0:T(8,128)} %copy.22, f32[256,16,8]{1,2,0:T(8,128)} %copy.25), kind=kOutput, calls=%fused_computation.63 | convolution fusion | flops 12582912 | bytes 917504 | tf_op jit(solution)/shard_map/while/body/eval_jaxpr/npa,npd->nad/dot_general | solution.py:309
  35.0 2.2 %copy.34 = f32[256,32,8]{0,2,1:T(8,128)} copy(f32[256,32,8]{1,2,0:T(8,128)} %fusion.47) | data formatting | bytes 524288 | tf_op jit(solution)/shard_map/while/body/eval_jaxpr/npa,npd->nad/dot_general | solution.py:309
  37.2 2.0 %fusion.13 = f32[250,256]{1,0:T(8,128)} fusion(f32[256,32,8]{0,2,1:T(8,128)} %copy.34, s32[256]{0:T(256)S(1)} %bitcast.90), kind=kOutput, calls=%fused_computation.22 | convolution fusion | flops 196736000 | bytes 519168 | tf_op jit(solution)/shard_map/while/body/eval_jaxpr/dot_general | solution.py:323
  39.3 1.7 %reshape.100 = f32[64000]{0:T(1024)} reshape(f32[250,256]{1,0:T(8,128)} %fusion.13) | data formatting | bytes 512000 | tf_op jit(solution)/shard_map/reshape | solution.py:335
  41.0 6.0 %fusion.44 = f32[256,16,32]{2,1,0:T(8,128)} fusion(f32[256,16,8]{1,2,0:T(8,128)} %copy.25, f32[256,32,8]{1,2,0:T(8,128)S(1)} %copy.23), kind=kOutput, calls=%fused_computation.60 | convolution fusion | flops 12582912 | bytes 917504 | tf_op jit(solution)/shard_map/while/body/eval_jaxpr/npd,nad->npa/dot_general | solution.py:310
  47.0 2.5 %copy.27 = f32[256,16,32]{0,2,1:T(8,128)S(1)} copy(f32[256,16,32]{2,1,0:T(8,128)} %fusion.44) | data formatting | bytes 1048576 | tf_op jit(solution)/shard_map/while/body/eval_jaxpr/npd,nad->npa/dot_general | solution.py:310
  49.7 8.5 %fusion.45 = f32[256,4,32]{2,1,0:T(4,128)S(1)} fusion(f32[256,4,128]{2,1,0:T(4,128)S(1)} %copy.28, f32[256,32,128]{2,1,0:T(8,128)} %bitcast.78), kind=kOutput, calls=%fused_computation.61 | convolution fusion | flops 50331648 | bytes 4849664 | tf_op jit(solution)/shard_map/while/body/eval_jaxpr/nib,nab->nia/dot_general | solution.py:313
  58.3 0.8 copy.29
  59.1 1.3 convolution_bitcast_fusion
  60.4 6.7 %fusion.46 = f32[256,32,128]{2,1,0:T(8,128)S(1)} fusion(f32[256,4,32]{2,1,0:T(4,128)S(1)} %copy.20, f32[256,4,128]{2,1,0:T(4,128)S(1)} %copy.28), kind=kOutput, calls=%fused_computation.62 | convolution fusion | flops 50331648 | bytes 4849664 | tf_op jit(solution)/shard_map/while/body/eval_jaxpr/nia,nib->nab/dot_general | solution.py:314
  67.1 4.7 %fusion.4 = f32[25,32,8,128]{3,2,1,0:T(8,128)S(1)} fusion(f32[32,8,32,128]{3,2,1,0:T(8,128)S(1)} %bitcast.79, s32[256]{0:T(256)S(1)} %bitcast.86), kind=kOutput, calls=%fused_computation.9 | convolution fusion | flops 2516633600 | bytes 7472128 | tf_op jit(solution)/shard_map/while/body/eval_jaxpr/dot_general | solution.py:323
  71.8 0.6 copy.37
  72.4 0.4 copy-done.2
  72.8 0.2 fusion.3.flat
  73.0 18.1 %pack.1.w = f32[2,2,2048,128]{3,2,1,0:T(8,128)S(1)} custom-call(f32[7104,128]{1,0:T(8,128)S(1)} %fusion.3.flat), custom_call_target="tpu_custom_call" | custom-call | tf_op jit(solution)/shard_map/pack/pallas_call | solution.py:248
  91.1 48.6 %exchange.1 = (f32[16,128]{1,0:T(8,128)S(1)}, f32[258,256]{1,0:T(8,128)S(1)}) custom-call(f32[2,2,2048,128]{3,2,1,0:T(8,128)S(1)} %pack.1.w, f32[2,256,128]{2,1,0:T(8,128)S(1)} %pad_maximum_fusion.t, f32[8,128]{1,0:T(8,128)S(1)} %pad.9.e), custom_call_target="tpu_custom_call" | custom-call | tf_op jit(solution)/shard_map/exchange/pallas_call | solution.py:220
  139.6 0.6 copy.46
  140.2 0.7 copy.47
  (34 shorter events, 1.5 us)
Async XLA Ops:
  0.6 3.1 %copy-start = (bf16[200,4096]{1,0:T(8,128)(2,1)S(1)}, bf16[200,4096]{1,0:T(8,128)(2,1)}, u32[]{:S(2)}) copy-start(bf16[200,4096]{1,0:T(8,128)(2,1)} %param.13) | copy-start | bytes 4915204
  6.0 1.9 %copy-start.1 = (f32[32,8,32,128]{3,2,1,0:T(8,128)}, f32[32,8,32,128]{3,2,1,0:T(8,128)S(1)}, u32[]{:S(2)}) copy-start(f32[32,8,32,128]{3,2,1,0:T(8,128)S(1)} %copy.35) | copy-start | bytes 12582916
  14.2 11.1 %copy-start.6 = (s32[1,256]{1,0:T(1,128)S(1)}, s32[1,256]{1,0:T(1,128)}, u32[]{:S(2)}) copy-start(s32[1,256]{1,0:T(1,128)} %param.20) | copy-start | bytes 3076
  14.3 11.4 %copy-start.3 = (bf16[256,256]{1,0:T(8,128)(2,1)S(1)}, bf16[256,256]{1,0:T(8,128)(2,1)}, u32[]{:S(2)}) copy-start(bf16[256,256]{1,0:T(8,128)(2,1)} %param.16) | copy-start | bytes 393220
  14.3 11.5 %copy-start.5 = (bf16[64,128]{1,0:T(8,128)(2,1)S(1)}, bf16[64,128]{1,0:T(8,128)(2,1)}, u32[]{:S(2)}) copy-start(bf16[64,128]{1,0:T(8,128)(2,1)} %param.15) | copy-start | bytes 49156
  14.3 11.5 %copy-start.9 = (f32[256]{0:T(256)S(1)}, f32[256]{0:T(256)}, u32[]{:S(2)}) copy-start(f32[256]{0:T(256)} %param.17) | copy-start | bytes 3076
  14.3 11.6 %copy-start.10 = (f32[256]{0:T(256)S(1)}, f32[256]{0:T(256)}, u32[]{:S(2)}) copy-start(f32[256]{0:T(256)} %param.18) | copy-start | bytes 3076
  14.3 11.6 %copy-start.11 = (s32[64]{0:T(128)S(1)}, s32[64]{0:T(128)}, u32[]{:S(2)}) copy-start(s32[64]{0:T(128)} %param.19) | copy-start | bytes 772
  27.7 9.6 %copy-start.7 = (s32[1,256]{1,0:T(1,128)S(1)}, s32[1,256]{1,0:T(1,128)}, u32[]{:S(2)}) copy-start(s32[1,256]{1,0:T(1,128)} %param.23) | copy-start | bytes 3076
  49.5 9.6 %copy-start.8 = (s32[1,256]{1,0:T(1,128)S(1)}, s32[1,256]{1,0:T(1,128)}, u32[]{:S(2)}) copy-start(s32[1,256]{1,0:T(1,128)} %param.21) | copy-start | bytes 3076
  58.3 8.9 %copy-start.4 = (s32[1,256]{1,0:T(1,128)S(1)}, s32[1,256]{1,0:T(1,128)}, u32[]{:S(2)}) copy-start(s32[1,256]{1,0:T(1,128)} %param.22) | copy-start | bytes 3076
  71.8 1.0 copy-start.2

commit v2 on v1

--- a/solution.py
+++ b/solution.py
@@ -6,31 +6,6 @@
 from jax.experimental import pallas as pl
 from jax.experimental.pallas import tpu as pltpu
 from jax.sharding import PartitionSpec as P
-
-D1 = 4
-D2 = 4
-D3 = 8
-R = 32
-
-
-def one_hot(digits, count, kind):
-    return (digits[:, None] == jnp.arange(count, dtype=jnp.int32)[None, :]).astype(kind)
-
-
-def slices(digits, core):
-    return jnp.dot(
-        one_hot(digits, core.shape[0], jnp.bfloat16), core, preferred_element_type=jnp.float32
-    )
-
-
-def factors(digits, cores):
-    high = lax.Precision.HIGHEST
-    first = slices(digits[0], cores[0]).reshape(-1, D1, R)
-    middle = slices(digits[1], cores[1]).reshape(-1, R, D2 * R)
-    last = slices(digits[2], cores[2]).reshape(-1, R, D3)
-    left = jnp.einsum("nia,nab->nib", first, middle, precision=high).reshape(-1, D1 * D2, R)
-    return (first, middle, last, left)
-
 
 MESH = pl.DeviceIdType.MESH
 ORDER = (1, 7, 2, 6, 3, 5, 4)
@@ -229,113 +204,145 @@
     )(w, t, e)
 
 
-def pack_kernel(flat, w):
-    def body(q, carry):
+def contract(a, b, left, right, **kw):
+    return lax.dot_general(a, b, (((left,), (right,)), ((), ())), preferred_element_type=jnp.float32, **kw)
+
+
+def halves(value):
+    high = value.astype(jnp.bfloat16)
+    return high, (value - high.astype(jnp.float32)).astype(jnp.bfloat16)
+
+
+def grads_kernel(one, two, three, dense, w_top, bias, w_out, labels, bags, digit_one, digit_two, digit_three,
+                 w, t, e, first, mid, last, turned, left, g, gl, gm, glast, flat, sided, gf):
+    bf16, f32 = jnp.bfloat16, jnp.float32
+    high = lax.Precision.HIGHEST
+
+    def hot(row, count, kind):
+        return (lax.broadcasted_iota(jnp.int32, (count, row.shape[1]), 0) == row).astype(kind)
+
+    hot_one = hot(digit_one[...], 200, bf16)
+    hot_two = hot(digit_two[...], 200, bf16)
+    hot_three = hot(digit_three[...], 250, bf16)
+    bag = hot(bags[...], 64, f32)
+    first[...] = contract(one[...], hot_one, 0, 0)
+    ends = contract(three[...], hot_three, 0, 0)
+    last[...] = ends
+    for side in range(2):
+        sided[side] = ends[:, side * 128:side * 128 + 128]
+        for d in range(8):
+            turned[d * 32:d * 32 + 32, side * 128:side * 128 + 128] = sided.at[side][pl.ds(d, 32, stride=8), :]
+    for part in range(8):
+        mid[part * 512:part * 512 + 512, :] = contract(two[:, part * 512:part * 512 + 512], hot_two, 0, 0)
+
+    for b in range(4):
+        sums = [jnp.zeros((32, 256), f32) for _ in range(4)]
+        for a in range(32):
+            piece = mid[a * 128 + b * 32:a * 128 + b * 32 + 32, :]
+            sums = [total + first[i * 32 + a:i * 32 + a + 1, :] * piece for i, total in enumerate(sums)]
+        for i in range(4):
+            left[(i * 4 + b) * 32:(i * 4 + b) * 32 + 32, :] = sums[i]
+    rows = []
+    for p in range(16):
+        total = jnp.zeros((8, 256), f32)
+        for a in range(32):
+            total = total + left[p * 32 + a:p * 32 + a + 1, :] * last[a * 8:a * 8 + 8, :]
+        rows.append(total)
+    embedded = jnp.concatenate(rows, axis=0)
+
+    pooled = contract(bag, embedded, 1, 1, precision=high)
+    joined = jnp.concatenate([dense[...], pooled.astype(bf16)], axis=1)
+    pre = jnp.dot(joined, w_top[...], preferred_element_type=f32) + bias[...]
+    sig = jax.nn.sigmoid(pre)
+    hidden = pre * sig
+    logit = jnp.sum(hidden * w_out[...], axis=1, keepdims=True)
+    square = lax.broadcasted_iota(jnp.int32, (64, 64), 0) == lax.broadcasted_iota(jnp.int32, (64, 64), 1)
+    label = jnp.sum(jnp.where(square, labels[...].astype(f32), 0.0), axis=1, keepdims=True)
+    dlogit = (jax.nn.sigmoid(logit) - label) / 64
+    dpre = dlogit * w_out[...] * (sig * (1.0 + pre * (1.0 - sig)))
+    low = dpre.astype(bf16)
+    weight = contract(joined, low, 0, 0)
+    t[0] = weight[:, 0:128]
+    t[1] = weight[:, 128:256]
+    grad_bias = jnp.sum(dpre, axis=0, keepdims=True)
+    grad_out = jnp.sum(hidden * dlogit, axis=0, keepdims=True)
+    e[...] = jnp.concatenate([grad_bias[:, :128], grad_bias[:, 128:], grad_out[:, :128], grad_out[:, 128:],
+                              jnp.zeros((4, 128), f32)], axis=0)
+    pooled_grad = contract(w_top[128:256, :], low, 1, 1)
+    g[...] = jnp.dot(pooled_grad, bag, precision=high, preferred_element_type=f32)
+
+    for a in range(32):
+        total = jnp.zeros((8, 256), f32)
+        for p in range(16):
+            total = total + left[p * 32 + a:p * 32 + a + 1, :] * g[p * 8:p * 8 + 8, :]
+        glast[a * 8:a * 8 + 8, :] = total
+    for p in range(16):
+        total = jnp.zeros((32, 256), f32)
+        for d in range(8):
+            total = total + g[p * 8 + d:p * 8 + d + 1, :] * turned[d * 32:d * 32 + 32, :]
+        gl[p * 32:p * 32 + 32, :] = total
+
+    def scatter(table, value):
+        upper, lower = halves(value)
+        return contract(table, upper, 1, 1) + contract(table, lower, 1, 1)
+
+    for a in range(0, 32, 2):
+        for half in range(2):
+            c = a + half
+            partial = [jnp.zeros((8, 256), f32) for _ in range(4)]
+            for b in range(16):
+                piece = mid[c * 128 + b * 8:c * 128 + b * 8 + 8, :]
+                total = jnp.zeros((8, 256), f32)
+                for i in range(4):
+                    slope = gl[i * 128 + b * 8:i * 128 + b * 8 + 8, :]
+                    total = total + first[i * 32 + c:i * 32 + c + 1, :] * slope
+                    partial[i] = partial[i] + slope * piece
+                gm[half * 128 + b * 8:half * 128 + b * 8 + 8, :] = total
+            for i in range(4):
+                for side in range(2):
+                    gf.at[side][pl.ds(i * 32 + c, 8, stride=128), :] = partial[i][:, side * 128:side * 128 + 128]
+        middle = scatter(hot_two, gm[...])
+        flat[pl.ds(200 + a, 200, stride=32), :] = middle[:, 0:128]
+        flat[pl.ds(201 + a, 200, stride=32), :] = middle[:, 128:256]
+    spread = scatter(hot_one, jnp.concatenate([gf[0], gf[1]], axis=1))
+    total = spread[:, 0:128]
+    for part in range(1, 8):
+        total = total + spread[:, part * 128:part * 128 + 128]
+    flat[7096:7104, :] = jnp.zeros((8, 128), f32)
+    flat[0:200, :] = total
+    ending = scatter(hot_three, glast[...])
+    flat[pl.ds(6600, 250, stride=2), :] = ending[:, 0:128]
+    flat[pl.ds(6601, 250, stride=2), :] = ending[:, 128:256]
+
+    for q in range(512):
         b, x, y = (q // 16) % 2, (q // 32) % 4, q % 8
         z = (q // 128) * 2 + (q // 8) % 2
-        u = (1 - b) * y + b * z
-        v = (1 - b) * z + b * y
-        rows = flat[pl.ds((1775 * q) // 128, 16), :]
-        w[b, 0, pl.ds(pl.multiple_of((x * 64 + u * 8 + v) * 8, 8), 8), :] = rows[0:8]
-        w[b, 1, pl.ds(pl.multiple_of((u * 32 + v * 4 + x) * 8, 8), 8), :] = rows[8:16]
-        return carry
-
-    lax.fori_loop(0, 512, body, 0)
-
-
-def pack(flat):
+        u, v = (y, z) if b == 0 else (z, y)
+        start = (1775 * q) // 128
+        w[b, 0, (x * 64 + u * 8 + v) * 8:(x * 64 + u * 8 + v) * 8 + 8, :] = flat[start:start + 8, :]
+        w[b, 1, (u * 32 + v * 4 + x) * 8:(u * 32 + v * 4 + x) * 8 + 8, :] = flat[start + 8:start + 16, :]
+
+
+def grads(*args):
+    f32 = jnp.float32
     vmem = pl.BlockSpec(memory_space=pltpu.VMEM)
+    rows = [128, 4096, 256, 256, 512, 128, 512, 256, 256]
     return pl.pallas_call(
-        pack_kernel,
-        out_shape=jax.ShapeDtypeStruct((2, 2, 2048, 128), jnp.float32),
-        in_specs=[vmem],
-        out_specs=vmem,
-        compiler_params=pltpu.CompilerParams(vmem_limit_bytes=20 * 1024 * 1024),
-        name="pack",
-    )(flat)
-
-
-def per_device(
-    core_one,
-    core_two,
-    core_three,
-    dense_rows,
-    w_top,
-    bias_top,
-    w_out,
-    labels,
-    bag_ids,
-    digit_one,
-    digit_two,
-    digit_three,
-):
-    high = lax.Precision.HIGHEST
-    cores = (core_one, core_two, core_three)
-    digits = jnp.stack([digit_one[0], digit_two[0], digit_three[0]])
-    looks = digits.shape[1]
-    block = min(256, looks)
-    blocks = looks // block
-    blocked = digits.reshape(3, blocks, block).transpose(1, 0, 2)
-    width = D1 * D2 * D3
-
-    def forward(carry, part):
-        first, middle, last, left = factors(part, cores)
-        return (carry, jnp.einsum("npa,nad->npd", left, last, precision=high).reshape(block, width))
-
-    _, embedded = lax.scan(forward, jnp.zeros((), jnp.float32), blocked)
-    embedded = embedded.reshape(looks, width)
-    samples = dense_rows.shape[0]
-    bag_table = one_hot(bag_ids[0], samples, jnp.float32)
-    pooled = jnp.dot(bag_table.T, embedded, precision=high)
-    joined = jnp.concatenate([dense_rows, pooled.astype(jnp.bfloat16)], axis=1)
-    pre = jnp.dot(joined, w_top, preferred_element_type=jnp.float32) + bias_top[None, :]
-    sig = jax.nn.sigmoid(pre)
-    hidden = pre * sig
-    logit = jnp.dot(hidden, w_out, precision=high)
-    dlogit = (jax.nn.sigmoid(logit) - labels.astype(jnp.float32)) / samples
-    dpre = dlogit[:, None] * w_out[None, :] * (sig * (1.0 + pre * (1.0 - sig)))
-    dpre_low = dpre.astype(jnp.bfloat16)
-    grad_weight = jnp.dot(joined.T, dpre_low, preferred_element_type=jnp.float32)
-    grad_bias = jnp.sum(dpre, axis=0)
-    grad_output = jnp.sum(hidden * dlogit[:, None], axis=0)
-    top_local = jnp.concatenate([grad_weight, grad_bias[None, :], grad_output[None, :]], axis=0)
-    grad_pooled = jnp.dot(dpre_low, w_top[width:].T, preferred_element_type=jnp.float32)
-    grad_embedded = jnp.dot(bag_table, grad_pooled, precision=high).reshape(blocks, block, width)
-
-    def backward(totals, inputs):
-        part, grad_block = inputs
-        first, middle, last, left = factors(part, cores)
-        grad_view = grad_block.reshape(block, D1 * D2, D3)
-        grad_last = jnp.einsum("npa,npd->nad", left, grad_view, precision=high)
-        grad_left = jnp.einsum("npd,nad->npa", grad_view, last, precision=high).reshape(
-            block, D1, D2 * R
-        )
-        grad_first = jnp.einsum("nib,nab->nia", grad_left, middle, precision=high)
-        grad_middle = jnp.einsum("nia,nib->nab", first, grad_left, precision=high)
-        pieces = (
-            grad_first.reshape(block, -1),
-            grad_middle.reshape(block, -1),
-            grad_last.reshape(block, -1),
-        )
-        updated = tuple(
-            (
-                total
-                + jnp.dot(
-                    one_hot(part[number], cores[number].shape[0], jnp.float32).T,
-                    pieces[number],
-                    precision=high,
-                )
-                for number, total in enumerate(totals)
-            )
-        )
-        return (updated, None)
-
-    start = tuple((jnp.zeros(core.shape, jnp.float32) for core in cores))
-    totals, _ = lax.scan(backward, start, (blocked, grad_embedded))
-    flat = jnp.concatenate([total.reshape(-1) for total in totals])
-    packed = pack(jnp.pad(flat, (0, 512)).reshape(7104, 128))
-    sides = jnp.stack([top_local[:256, :128], top_local[:256, 128:]])
-    extra = jnp.pad(top_local[256:].reshape(4, 128), ((0, 4), (0, 0)))
+        grads_kernel,
+        out_shape=(jax.ShapeDtypeStruct((2, 2, 2048, 128), f32), jax.ShapeDtypeStruct((2, 256, 128), f32),
+                   jax.ShapeDtypeStruct((8, 128), f32)),
+        in_specs=[vmem] * len(args),
+        out_specs=(vmem,) * 3,
+        scratch_shapes=[pltpu.VMEM((count, 256), f32) for count in rows] + [pltpu.VMEM((7104, 128), f32), pltpu.VMEM((2, 256, 128), f32), pltpu.VMEM((2, 1024, 128), f32)],
+        compiler_params=pltpu.CompilerParams(vmem_limit_bytes=50 * 1024 * 1024),
+        name="grads",
+    )(*args)
+
+
+def per_device(core_one, core_two, core_three, dense_rows, w_top, bias_top, w_out, labels, bag_ids, digit_one, digit_two,
+               digit_three):
+    packed, sides, extra = grads(core_one, core_two, core_three, dense_rows, w_top, bias_top[None], w_out[None], labels[None],
+                                 bag_ids, digit_one, digit_two, digit_three)
     chunk, top_grad = exchange(packed, sides, extra)
     return (chunk.reshape(-1)[:1775], top_grad)
 

time: 142 us -> 76.9 us (0.54)
  matrix products: 50.4 us -> 0 us
  local copies, waits for them, and re-layouts: 22.6 us -> 13 us
  Pallas kernels: 66.6 us -> 62.8 us
    dot_general x18 -> x0, matrix products: 50.4 us -> none  [the longest x1 8.54 us: backward(): grad_first = jnp.einsum('nib,nab->nia', grad_left, middle, precision=high)]
    dot_general x5 -> x0, local copies, waits for them, and re-layouts: 9.19 us -> none  [the longest x1 2.49 us: backward(): jnp.einsum('npd,nad->npa', grad_view, last, precision=high)]
    reshape x7 -> x0, local copies, waits for them, and re-layouts: 8.41 us -> none  [the longest x1 3.6 us: factors(): jnp.einsum('nia,nab->nib', first, middle, precision=high)]
    unnamed x28, local copies, waits for them, and re-layouts: 5 us -> 13 us
    pallas_call x1, Pallas kernels: 18.1 us -> 14.2 us  [grads(): pl.pallas_call(grads_kernel, out_shape=(jax.ShapeDtypeStruct((2, 2, 2048,...]
where the time goes in v2:
time: 76.9 us; the launch traced here: 76.4 us
  Pallas kernels  62.8 us (82%)
  local copies, waits for them, and re-layouts  13 us (17%)
    pallas_call x1, Pallas kernels, exchange(): pl.pallas_call(exchange_kernel, out_shape=(jax.ShapeDtypeStruct((16, 128)...  48.6 us
    pallas_call x1, Pallas kernels, grads(): pl.pallas_call(grads_kernel, out_shape=(jax.ShapeDtypeStruct((2, 2, 2048,...  14.2 us
    unnamed x28, local copies, waits for them, and re-layouts  13 us

profile of v2, /device:TPU:1, one launch (start us, length us, event | category | flops | bytes accessed | tf_op | source)
XLA Modules:
  0.0 76.4 jit_solution(5464666362214301316)
XLA Ops:
  0.6 0.0 copy-start.1
  0.6 1.4 %copy-done.1 = bf16[200,4096]{1,0:T(8,128)(2,1)S(1)} copy-done((bf16[200,4096]{1,0:T(8,128)(2,1)S(1)}, bf16[200,4096]{1,0:T(8,128)(2,1)}, u32[]{:S(2)}) %copy-start.1) | copy-done | bytes 1638424
  2.1 0.0 copy-start.2
  2.1 0.9 %copy-done.2 = bf16[250,256]{1,0:T(8,128)(2,1)S(1)} copy-done((bf16[250,256]{1,0:T(8,128)(2,1)S(1)}, bf16[250,256]{1,0:T(8,128)(2,1)}, u32[]{:S(2)}) %copy-start.2) | copy-done | bytes 128024
  3.0 0.0 copy-start.3
  3.0 0.9 %copy-done.3 = bf16[256,256]{1,0:T(8,128)(2,1)S(1)} copy-done((bf16[256,256]{1,0:T(8,128)(2,1)S(1)}, bf16[256,256]{1,0:T(8,128)(2,1)}, u32[]{:S(2)}) %copy-start.3) | copy-done | bytes 131096
  3.9 0.0 copy-start.4
  3.9 0.8 %copy-done.4 = bf16[200,128]{1,0:T(8,128)(2,1)S(1)} copy-done((bf16[200,128]{1,0:T(8,128)(2,1)S(1)}, bf16[200,128]{1,0:T(8,128)(2,1)}, u32[]{:S(2)}) %copy-start.4) | copy-done | bytes 51224
  4.7 0.0 copy-start.5
  4.7 0.7 copy-done.5
  5.4 0.0 copy-start.6
  5.4 0.7 copy-done.6
  6.1 0.0 copy-start.7
  6.1 0.7 copy-done.7
  6.8 0.0 copy-start.8
  6.8 0.7 copy-done.8
  7.4 0.0 copy-start.9
  7.4 0.7 copy-done.9
  8.1 0.0 copy-start.10
  8.1 0.7 copy-done.10
  8.8 0.0 copy-start.11
  8.8 0.7 copy-done.11
  9.5 0.0 copy-start.12
  9.5 0.7 copy-done.12
  10.1 14.2 %grads.1 = (f32[2,2,2048,128]{3,2,1,0:T(8,128)}, f32[2,256,128]{2,1,0:T(8,128)S(1)}, f32[8,128]{1,0:T(8,128)S(1)}) custom-call(bf16[200,128]{1,0:T(8,128)(2,1)S(1)} %copy-done.4, bf16[200,4096]{1,0:T(8,128)(2,1)S(1)} %copy-done.1, bf16[250,256]{1,0:T(8,128)(2,1)S(1)} %copy-done.2, bf16[64,128]{1,0:T(8,128)(2,1)S(1)} %copy-done.5, ...), custom_call_target="tpu_custom_call" | custom-call | tf_op jit(solution)/shard_map/grads/pallas_call | solution.py:330
  24.4 0.0 copy-start
  24.4 2.2 %copy-done = f32[2,2,2048,128]{3,2,1,0:T(8,128)S(1)} copy-done((f32[2,2,2048,128]{3,2,1,0:T(8,128)S(1)}, f32[2,2,2048,128]{3,2,1,0:T(8,128)}, u32[]{:S(2)}) %copy-start) | copy-done | bytes 4194328
  26.6 48.6 %exchange.1 = (f32[16,128]{1,0:T(8,128)S(1)}, f32[258,256]{1,0:T(8,128)S(1)}) custom-call(f32[2,2,2048,128]{3,2,1,0:T(8,128)S(1)} %copy-done, f32[2,256,128]{2,1,0:T(8,128)S(1)} %get-tuple-element.8.t, f32[8,128]{1,0:T(8,128)S(1)} %get-tuple-element.9.e), custom_call_target="tpu_custom_call" | custom-call | tf_op jit(solution)/shard_map/exchange/pallas_call | solution.py:195
  75.1 0.6 copy.16
  75.7 0.7 copy.17
Async XLA Ops:
  0.6 1.4 %copy-start.1 = (bf16[200,4096]{1,0:T(8,128)(2,1)S(1)}, bf16[200,4096]{1,0:T(8,128)(2,1)}, u32[]{:S(2)}) copy-start(bf16[200,4096]{1,0:T(8,128)(2,1)} %two.1) | copy-start | bytes 4915204
  2.1 0.9 %copy-start.2 = (bf16[250,256]{1,0:T(8,128)(2,1)S(1)}, bf16[250,256]{1,0:T(8,128)(2,1)}, u32[]{:S(2)}) copy-start(bf16[250,256]{1,0:T(8,128)(2,1)} %three.1) | copy-start | bytes 384004
  3.0 0.9 %copy-start.3 = (bf16[256,256]{1,0:T(8,128)(2,1)S(1)}, bf16[256,256]{1,0:T(8,128)(2,1)}, u32[]{:S(2)}) copy-start(bf16[256,256]{1,0:T(8,128)(2,1)} %w_top.1) | copy-start | bytes 393220
  3.9 0.8 %copy-start.4 = (bf16[200,128]{1,0:T(8,128)(2,1)S(1)}, bf16[200,128]{1,0:T(8,128)(2,1)}, u32[]{:S(2)}) copy-start(bf16[200,128]{1,0:T(8,128)(2,1)} %one.1) | copy-start | bytes 153604
  4.7 0.7 copy-start.5
  5.4 0.7 copy-start.6
  6.1 0.7 copy-start.7
  6.8 0.7 copy-start.8
  7.4 0.7 copy-start.9
  8.1 0.7 copy-start.10
  8.8 0.7 copy-start.11
  9.5 0.7 copy-start.12
  24.4 2.2 %copy-start = (f32[2,2,2048,128]{3,2,1,0:T(8,128)S(1)}, f32[2,2,2048,128]{3,2,1,0:T(8,128)}, u32[]{:S(2)}) copy-start(f32[2,2,2048,128]{3,2,1,0:T(8,128)} %get-tuple-element.7.w) | copy-start | bytes 12582916

commit v3 on v1

v3 whole, which is shorter than its diff:
```python
import functools

import jax
import jax.numpy as jnp
from jax import lax
from jax.experimental import pallas as pl
from jax.experimental.pallas import tpu as pltpu
from jax.sharding import PartitionSpec as P

MESH = pl.DeviceIdType.MESH
ORDER = (1, 7, 2, 6, 3, 5, 4)
XORDER = (1, 3, 2)


def whereabouts():
    gx, gy = lax.axis_index("gx"), lax.axis_index("gy")
    core, x = gx % 2, (gx // 2) % 4
    y, z = gy % 8, (gx // 8) * 2 + gy // 8
    u = (1 - core) * y + core * z
    v = (1 - core) * z + core * y
    return core, x, u, v


def place(core, x, u, v):
    y = (1 - core) * u + core * v
    z = core * u + (1 - core) * v
    return ((z // 2) * 8 + x * 2 + core, (z % 2) * 8 + y)


def summed(rows, step, store, *parts):
    def body(i, carry):
        at = pl.ds(pl.multiple_of(i * step, step), step)
        total = parts[0](at)
        for part in parts[1:]:
            total = total + part(at)
        store(at, total)
        return carry

    lax.fori_loop(0, rows // step, body, 0)


def contract(a, b, left, right, **kw):
    return lax.dot_general(a, b, (((left,), (right,)), ((), ())), preferred_element_type=jnp.float32, **kw)


def halves(value):
    high = value.astype(jnp.bfloat16)
    return high, (value - high.astype(jnp.float32)).astype(jnp.bfloat16)


def step_kernel(*refs):
    sources, (out, top), rest = refs[:12], refs[12:14], refs[14:]
    inputs, sems, rest = rest[:12], rest[12], rest[13:]
    one, two, three, dense, w_top, bias, w_out, labels, bags, digit_one, digit_two, digit_three = inputs
    (w, t, e, first, mid, last, turned, left, g, gl, gm, glast, flat, sided, gf) = rest[:15]
    (r0, s1, r1a, r1b, s2a, s2b, r2a, r2b, s3a, s3b, r3a, r3b, rt0, re0, st1, rt1, st2, rt2, rt3, g1, g2, g3,
     send, recv) = rest[15:]
    loads = [pltpu.make_async_copy(sources[i], inputs[i], sems.at[i]) for i in range(12)]
    for i in (9, 11, 10, 0, 2, 1, 8, 3, 4, 5, 6, 7):
        loads[i].start()
    core, x, u, v = whereabouts()
    y = (1 - core) * u + core * v
    z = core * u + (1 - core) * v
    mate = ((z // 2) * 8 + x * 2 + (1 - core), (z % 2) * 8 + y)
    other_x = {k: place(core, (x + k) % 4, u, v) for k in XORDER}
    other_u = {k: place(core, x, (u + k) % 8, v) for k in ORDER}
    other_v = {k: place(core, x, u, (v + k) % 8) for k in ORDER}
    barrier = pltpu.get_barrier_semaphore()
    peers = [mate] + list(other_x.values()) + list(other_u.values()) + list(other_v.values())
    for peer in peers:
        pl.semaphore_signal(barrier, inc=1, device_id=peer, device_id_type=MESH)
    copies = []

    def put(src, dst, peer):
        spot = len(copies)
        copy = pltpu.make_async_remote_copy(
            src_ref=src, dst_ref=dst, send_sem=send.at[spot], recv_sem=recv.at[spot],
            device_id=peer, device_id_type=MESH)
        copy.start()
        copies.append(copy)
        return copy

    def arrived(group):
        for copy in group:
            copy.wait_recv()

    for load in loads:
        load.wait()

    bf16, f32 = jnp.bfloat16, jnp.float32
    high = lax.Precision.HIGHEST

    def hot(row, count, kind):
        return (lax.broadcasted_iota(jnp.int32, (count, row.shape[1]), 0) == row).astype(kind)

    hot_one = hot(digit_one[...], 200, bf16)
    hot_two = hot(digit_two[...], 200, bf16)
    hot_three = hot(digit_three[...], 250, bf16)
    bag = hot(bags[...], 64, f32)
    first[...] = contract(one[...], hot_one, 0, 0)
    ends = contract(three[...], hot_three, 0, 0)
    last[...] = ends
    for side in range(2):
        sided[side] = ends[:, side * 128:side * 128 + 128]
        for d in range(8):
            turned[d * 32:d * 32 + 32, side * 128:side * 128 + 128] = sided.at[side][pl.ds(d, 32, stride=8), :]
    for part in range(8):
        mid[part * 512:part * 512 + 512, :] = contract(two[:, part * 512:part * 512 + 512], hot_two, 0, 0)

    for b in range(4):
        sums = [jnp.zeros((32, 256), f32) for _ in range(4)]
        for a in range(32):
            piece = mid[a * 128 + b * 32:a * 128 + b * 32 + 32, :]
            sums = [total + first[i * 32 + a:i * 32 + a + 1, :] * piece for i, total in enumerate(sums)]
        for i in range(4):
            left[(i * 4 + b) * 32:(i * 4 + b) * 32 + 32, :] = sums[i]
    rows = []
    for p in range(16):
        total = jnp.zeros((8, 256), f32)
        for a in range(32):
            total = total + left[p * 32 + a:p * 32 + a + 1, :] * last[a * 8:a * 8 + 8, :]
        rows.append(total)
    embedded = jnp.concatenate(rows, axis=0)

    pooled = contract(bag, embedded, 1, 1, precision=high)
    joined = jnp.concatenate([dense[...], pooled.astype(bf16)], axis=1)
    pre = jnp.dot(joined, w_top[...], preferred_element_type=f32) + bias[...]
    sig = jax.nn.sigmoid(pre)
    hidden = pre * sig
    logit = jnp.sum(hidden * w_out[...], axis=1, keepdims=True)
    square = lax.broadcasted_iota(jnp.int32, (64, 64), 0) == lax.broadcasted_iota(jnp.int32, (64, 64), 1)
    label = jnp.sum(jnp.where(square, labels[...].astype(f32), 0.0), axis=1, keepdims=True)
    dlogit = (jax.nn.sigmoid(logit) - label) / 64
    dpre = dlogit * w_out[...] * (sig * (1.0 + pre * (1.0 - sig)))
    low = dpre.astype(bf16)
    weight = contract(joined, low, 0, 0)
    t[0] = weight[:, 0:128]
    t[1] = weight[:, 128:256]
    grad_bias = jnp.sum(dpre, axis=0, keepdims=True)
    grad_out = jnp.sum(hidden * dlogit, axis=0, keepdims=True)
    e[...] = jnp.concatenate([grad_bias[:, :128], grad_bias[:, 128:], grad_out[:, :128], grad_out[:, 128:],
                              jnp.zeros((4, 128), f32)], axis=0)
    pooled_grad = contract(w_top[128:256, :], low, 1, 1)
    g[...] = jnp.dot(pooled_grad, bag, precision=high, preferred_element_type=f32)

    pl.semaphore_wait(barrier, len(peers))
    t0 = [put(t.at[1 - core], rt0, mate), put(e, re0, mate)]

    for a in range(32):
        total = jnp.zeros((8, 256), f32)
        for p in range(16):
            total = total + left[p * 32 + a:p * 32 + a + 1, :] * g[p * 8:p * 8 + 8, :]
        glast[a * 8:a * 8 + 8, :] = total
    for p in range(16):
        total = jnp.zeros((32, 256), f32)
        for d in range(8):
            total = total + g[p * 8 + d:p * 8 + d + 1, :] * turned[d * 32:d * 32 + 32, :]
        gl[p * 32:p * 32 + 32, :] = total

    def scatter(table, value):
        upper, lower = halves(value)
        return contract(table, upper, 1, 1) + contract(table, lower, 1, 1)

    for a in range(0, 32, 2):
        for half in range(2):
            c = a + half
            partial = [jnp.zeros((8, 256), f32) for _ in range(4)]
            for b in range(16):
                piece = mid[c * 128 + b * 8:c * 128 + b * 8 + 8, :]
                total = jnp.zeros((8, 256), f32)
                for i in range(4):
                    slope = gl[i * 128 + b * 8:i * 128 + b * 8 + 8, :]
                    total = total + first[i * 32 + c:i * 32 + c + 1, :] * slope
                    partial[i] = partial[i] + slope * piece
                gm[half * 128 + b * 8:half * 128 + b * 8 + 8, :] = total
            for i in range(4):
                for side in range(2):
                    gf.at[side][pl.ds(i * 32 + c, 8, stride=128), :] = partial[i][:, side * 128:side * 128 + 128]
        middle = scatter(hot_two, gm[...])
        flat[pl.ds(200 + a, 200, stride=32), :] = middle[:, 0:128]
        flat[pl.ds(201 + a, 200, stride=32), :] = middle[:, 128:256]
    spread = scatter(hot_one, jnp.concatenate([gf[0], gf[1]], axis=1))
    total = spread[:, 0:128]
    for part in range(1, 8):
        total = total + spread[:, part * 128:part * 128 + 128]
    flat[7096:7104, :] = jnp.zeros((8, 128), f32)
    flat[0:200, :] = total
    ending = scatter(hot_three, glast[...])
    flat[pl.ds(6600, 250, stride=2), :] = ending[:, 0:128]
    flat[pl.ds(6601, 250, stride=2), :] = ending[:, 128:256]

    for q in range(512):
        side, qx, qy = (q // 16) % 2, (q // 32) % 4, q % 8
        qz = (q // 128) * 2 + (q // 8) % 2
        qu, qv = (qy, qz) if side == 0 else (qz, qy)
        start, upper_at, lower_at = (1775 * q) // 128, (qx * 64 + qu * 8 + qv) * 8, (qu * 32 + qv * 4 + qx) * 8
        w[side, 0, upper_at:upper_at + 8, :] = flat[start:start + 8, :]
        w[side, 1, lower_at:lower_at + 8, :] = flat[start + 8:start + 16, :]

    p0 = [put(w.at[1 - core, color], r0.at[color], mate) for color in (0, 1)]
    arrived(t0)
    extra = e[...] + re0[...]
    for part in range(4):
        rows = pl.ds(part * 64, 64)
        st1[part, 0:64, :] = t[core, rows, :] + rt0[rows, :]
        st1[part, 64:72, :] = extra
    t1 = [put(st1.at[(x + k) % 4], rt1.at[x], other_x[k]) for k in XORDER]
    rt1[x] = st1[x]


    def fold(color):
        def store(at, value):
            s1[color, at, :] = value
        summed(2048, 256, store, lambda at: w[core, color, at, :], lambda at: r0[color, at, :])

    arrived(p0[:1])
    fold(0)
    p1a = [put(s1.at[0, pl.ds(((x + k) % 4) * 512, 512)], r1a.at[k - 1], other_x[k]) for k in XORDER]
    arrived(p0[1:])
    fold(1)
    p1b = [put(s1.at[1, pl.ds(((u + k) % 8) * 256, 256)], r1b.at[k - 1], other_u[k]) for k in ORDER]

    arrived(t1)
    total = rt1[0]
    for part in range(1, 4):
        total = total + rt1[part]
    for part in range(8):
        st2[part, 0:8, :] = total[part * 8:part * 8 + 8]
        st2[part, 8:16, :] = total[64:72]
    t2 = [put(st2.at[(v + k) % 8], rt2.at[v], other_v[k]) for k in ORDER]
    rt2[v] = st2[v]
    arrived(t2)
    total = rt2[0]
    for part in range(1, 8):
        total = total + rt2[part]
    rt3[u] = total
    t3 = [put(rt3.at[u], rt3.at[u], other_u[k]) for k in ORDER]

    arrived(p1a)

    def store2a(at, value):
        s2a[at, :] = value

    summed(512, 128, store2a, lambda at: s1[0, pl.ds(x * 512 + at.start, at.size), :],
           *[functools.partial(lambda k, at: r1a[k, at, :], k) for k in range(3)])
    p2a = [put(s2a.at[pl.ds(((u + k) % 8) * 64, 64)], r2a.at[k - 1], other_u[k]) for k in ORDER]
    arrived(p1b)

    def store2b(at, value):
        s2b[at, :] = value

    summed(256, 64, store2b, lambda at: s1[1, pl.ds(u * 256 + at.start, at.size), :],
           *[functools.partial(lambda k, at: r1b[k, at, :], k) for k in range(7)])
    p2b = [put(s2b.at[pl.ds(((v + k) % 8) * 32, 32)], r2b.at[k - 1], other_v[k]) for k in ORDER]

    arrived(t3)
    total = rt3[0]
    for part in range(1, 8):
        total = total + rt3[part]
    g1[v] = total[0:8]
    extra = total[8:16]
    t4 = [put(g1.at[v], g1.at[v], other_v[k]) for k in ORDER]

    arrived(p2a)
    total = s2a[pl.ds(u * 64, 64), :]
    for part in range(7):
        total = total + r2a[part]
    s3a[...] = total
    p3a = [put(s3a.at[pl.ds(((v + k) % 8) * 8, 8)], r3a.at[k - 1], other_v[k]) for k in ORDER]
    arrived(p2b)
    total = s2b[pl.ds(v * 32, 32), :]
    for part in range(7):
        total = total + r2b[part]
    s3b[...] = total
    p3b = [put(s3b.at[pl.ds(((x + k) % 4) * 8, 8)], r3b.at[k - 1], other_x[k]) for k in XORDER]

    arrived(t4)
    g2[x] = g1[...]
    t5 = [put(g2.at[x], g2.at[x], other_x[k]) for k in XORDER]
    for copy in t5:
        copy.wait_recv()
    t6 = put(g2, g3, mate)

    arrived(p3a)
    upper = s3a[pl.ds(v * 8, 8), :]
    for part in range(7):
        upper = upper + r3a[part]
    arrived(p3b)
    lower = s3b[pl.ds(x * 8, 8), :]
    for part in range(3):
        lower = lower + r3b[part]
    gx, gy = lax.axis_index("gx"), lax.axis_index("gy")
    offset = ((gx * 16 + gy) * 1775) % 128
    turned = pltpu.roll(jnp.concatenate([upper, lower], axis=0), (128 - offset) % 128, 1)
    below = pltpu.roll(turned, 15, 0)
    lane = lax.broadcasted_iota(jnp.int32, (16, 128), 1)
    out[...] = jnp.where(lane < 128 - offset, turned, below)

    top[256:257, 0:128] = extra[0:1]
    top[256:257, 128:256] = extra[1:2]
    top[257:258, 0:128] = extra[2:3]
    top[257:258, 128:256] = extra[3:4]
    arrived([t6])

    @pl.when(core == 0)
    def _():
        top[0:256, 0:128] = g2[...].reshape(256, 128)
        top[0:256, 128:256] = g3[...].reshape(256, 128)

    @pl.when(core == 1)
    def _():
        top[0:256, 128:256] = g2[...].reshape(256, 128)
        top[0:256, 0:128] = g3[...].reshape(256, 128)

    for copy in copies:
        copy.wait_send()


def step(*args):
    bf16, f32, i32 = jnp.bfloat16, jnp.float32, jnp.int32
    kinds = [jax.typeof(arg) for arg in args]
    vmem = pl.BlockSpec(memory_space=pltpu.VMEM)
    wide = [128, 4096, 256, 256, 512, 128, 512, 256, 256]
    shapes = [(2, 2048), (2, 2048), (3, 512), (7, 256), (512,), (256,), (7, 64), (7, 32), (64,), (32,), (7, 8), (3, 8),
              (256,), (8,), (4, 72), (4, 72), (8, 16), (8, 16), (8, 16), (8, 8), (4, 8, 8), (4, 8, 8)]
    scratch = [pltpu.VMEM(kind.shape, kind.dtype) for kind in kinds] + [pltpu.SemaphoreType.DMA((12,))]
    scratch += [pltpu.VMEM(shape + (128,), f32) for shape in ((2, 2, 2048), (2, 256), (8,))]
    scratch += [pltpu.VMEM((count, 256), f32) for count in wide]
    scratch += [pltpu.VMEM(shape + (128,), f32) for shape in [(7104,), (2, 256), (2, 1024)] + shapes]
    scratch += [pltpu.SemaphoreType.DMA((70,)), pltpu.SemaphoreType.DMA((70,))]
    return pl.pallas_call(
        step_kernel,
        out_shape=(jax.ShapeDtypeStruct((16, 128), f32), jax.ShapeDtypeStruct((258, 256), f32)),
        in_specs=[pl.BlockSpec(memory_space=pl.ANY)] * 12,
        out_specs=(vmem, vmem),
        scratch_shapes=scratch,
        compiler_params=pltpu.CompilerParams(collective_id=0, has_side_effects=True, vmem_limit_bytes=36 * 1024 * 1024),
        name="step",
    )(*args)


def per_device(core_one, core_two, core_three, dense_rows, w_top, bias_top, w_out, labels, bag_ids, digit_one, digit_two,
               digit_three):
    chunk, top_grad = step(core_one, core_two, core_three, dense_rows, w_top, bias_top[None], w_out[None], labels[None],
                           bag_ids, digit_one, digit_two, digit_three)
    return (chunk.reshape(-1)[:1775], top_grad)


def solution(mesh):
    return jax.shard_map(
        per_device,
        mesh=mesh,
        in_specs=(
            P(),
            P(),
            P(),
            P(("gx", "gy"), None),
            P(),
            P(),
            P(),
            P(("gx", "gy")),
            P(("gx", "gy"), None),
            P(("gx", "gy"), None),
            P(("gx", "gy"), None),
            P(("gx", "gy"), None),
        ),
        out_specs=(P(("gx", "gy")), P()),
        check_vma=False,
    )
```

time: 142 us -> 68.6 us (0.48)
  matrix products: 50.4 us -> 0 us
  local copies, waits for them, and re-layouts: 22.6 us -> 10.8 us
  Pallas kernels: 66.6 us -> 56.7 us
    dot_general x18 -> x0, matrix products: 50.4 us -> none  [the longest x1 8.54 us: backward(): grad_first = jnp.einsum('nib,nab->nia', grad_left, middle, precision=high)]
    pallas_call x2 -> x1, Pallas kernels: 66.6 us -> 56.7 us  [step(): pl.pallas_call(step_kernel, out_shape=(jax.ShapeDtypeStruct((16, 128), f3...]
    dot_general x5 -> x0, local copies, waits for them, and re-layouts: 9.19 us -> none  [the longest x1 2.49 us: backward(): jnp.einsum('npd,nad->npa', grad_view, last, precision=high)]
    reshape x7 -> x0, local copies, waits for them, and re-layouts: 8.41 us -> none  [the longest x1 3.6 us: factors(): jnp.einsum('nia,nab->nib', first, middle, precision=high)]
    unnamed x28 -> x26, local copies, waits for them, and re-layouts: 5 us -> 10.8 us
where the time goes in v3:
time: 68.6 us; the launch traced here: 68.2 us
  Pallas kernels  56.7 us (83%)
  local copies, waits for them, and re-layouts  10.8 us (16%)
    pallas_call x1, Pallas kernels, step(): pl.pallas_call(step_kernel, out_shape=(jax.ShapeDtypeStruct((16, 128), f3...  56.7 us
    unnamed x26, local copies, waits for them, and re-layouts  10.8 us

profile of v3, /device:TPU:1, one launch (start us, length us, event | category | flops | bytes accessed | tf_op | source)
XLA Modules:
  0.0 68.2 jit_solution(18382511182731663889)
XLA Ops:
  0.6 0.0 copy-start
  0.6 1.4 %copy-done = bf16[200,4096]{1,0:T(8,128)(2,1)S(1)} copy-done((bf16[200,4096]{1,0:T(8,128)(2,1)S(1)}, bf16[200,4096]{1,0:T(8,128)(2,1)}, u32[]{:S(2)}) %copy-start) | copy-done | bytes 1638424
  2.1 0.0 copy-start.1
  2.1 0.9 %copy-done.1 = bf16[250,256]{1,0:T(8,128)(2,1)S(1)} copy-done((bf16[250,256]{1,0:T(8,128)(2,1)S(1)}, bf16[250,256]{1,0:T(8,128)(2,1)}, u32[]{:S(2)}) %copy-start.1) | copy-done | bytes 128024
  3.0 0.0 copy-start.2
  3.0 0.9 %copy-done.2 = bf16[256,256]{1,0:T(8,128)(2,1)S(1)} copy-done((bf16[256,256]{1,0:T(8,128)(2,1)S(1)}, bf16[256,256]{1,0:T(8,128)(2,1)}, u32[]{:S(2)}) %copy-start.2) | copy-done | bytes 131096
  3.9 0.0 copy-start.3
  3.9 0.8 %copy-done.3 = bf16[200,128]{1,0:T(8,128)(2,1)S(1)} copy-done((bf16[200,128]{1,0:T(8,128)(2,1)S(1)}, bf16[200,128]{1,0:T(8,128)(2,1)}, u32[]{:S(2)}) %copy-start.3) | copy-done | bytes 51224
  4.7 0.0 copy-start.4
  4.7 0.7 %copy-done.4 = bf16[64,128]{1,0:T(8,128)(2,1)S(1)} copy-done((bf16[64,128]{1,0:T(8,128)(2,1)S(1)}, bf16[64,128]{1,0:T(8,128)(2,1)}, u32[]{:S(2)}) %copy-start.4) | copy-done | bytes 16408
  5.4 0.0 copy-start.5
  5.4 0.7 copy-done.5
  6.1 0.0 copy-start.6
  6.1 0.7 copy-done.6
  6.8 0.0 copy-start.7
  6.8 0.7 copy-done.7
  7.4 0.0 copy-start.8
  7.4 0.7 copy-done.8
  8.1 0.0 copy-start.9
  8.1 0.7 copy-done.9
  8.8 0.0 copy-start.10
  8.8 0.7 copy-done.10
  9.5 0.0 copy-start.11
  9.5 0.7 copy-done.11
  10.1 56.7 %step.1 = (f32[16,128]{1,0:T(8,128)S(1)}, f32[258,256]{1,0:T(8,128)S(1)}) custom-call(bf16[200,128]{1,0:T(8,128)(2,1)S(1)} %copy-done.3, bf16[200,4096]{1,0:T(8,128)(2,1)S(1)} %copy-done, bf16[250,256]{1,0:T(8,128)(2,1)S(1)} %copy-done.1, bf16[64,128]{1,0:T(8,128)(2,1)S(1)} %copy-done.4, bf16[256,256]{1,0:T(8,128)(2,1)S(1)} %copy-done.2, ...), custom_call_target="tpu_custom_call" | custom-call | tf_op jit(solution)/shard_map/step/pallas_call | solution.py:331
  66.9 0.6 copy.16
  67.5 0.7 %copy.17 = f32[258,256]{1,0:T(8,128)} copy(f32[258,256]{1,0:T(8,128)S(1)} %get-tuple-element.9) | data formatting | bytes 528384
Async XLA Ops:
  0.6 1.4 %copy-start = (bf16[200,4096]{1,0:T(8,128)(2,1)S(1)}, bf16[200,4096]{1,0:T(8,128)(2,1)}, u32[]{:S(2)}) copy-start(bf16[200,4096]{1,0:T(8,128)(2,1)} %refs_1_.1) | copy-start | bytes 4915204
  2.1 0.9 %copy-start.1 = (bf16[250,256]{1,0:T(8,128)(2,1)S(1)}, bf16[250,256]{1,0:T(8,128)(2,1)}, u32[]{:S(2)}) copy-start(bf16[250,256]{1,0:T(8,128)(2,1)} %refs_2_.1) | copy-start | bytes 384004
  3.0 0.9 %copy-start.2 = (bf16[256,256]{1,0:T(8,128)(2,1)S(1)}, bf16[256,256]{1,0:T(8,128)(2,1)}, u32[]{:S(2)}) copy-start(bf16[256,256]{1,0:T(8,128)(2,1)} %refs_4_.1) | copy-start | bytes 393220
  3.9 0.8 %copy-start.3 = (bf16[200,128]{1,0:T(8,128)(2,1)S(1)}, bf16[200,128]{1,0:T(8,128)(2,1)}, u32[]{:S(2)}) copy-start(bf16[200,128]{1,0:T(8,128)(2,1)} %refs_0_.1) | copy-start | bytes 153604
  4.7 0.7 %copy-start.4 = (bf16[64,128]{1,0:T(8,128)(2,1)S(1)}, bf16[64,128]{1,0:T(8,128)(2,1)}, u32[]{:S(2)}) copy-start(bf16[64,128]{1,0:T(8,128)(2,1)} %refs_3_.1) | copy-start | bytes 49156
  5.4 0.7 copy-start.5
  6.1 0.7 copy-start.6
  6.8 0.7 copy-start.7
  7.4 0.7 copy-start.8
  8.1 0.7 copy-start.9
  8.8 0.7 copy-start.10
  9.5 0.7 copy-start.11

commit v4 on v3

--- a/solution.py
+++ b/solution.py
@@ -53,7 +53,7 @@
     inputs, sems, rest = rest[:12], rest[12], rest[13:]
     one, two, three, dense, w_top, bias, w_out, labels, bags, digit_one, digit_two, digit_three = inputs
     (w, t, e, first, mid, last, turned, left, g, gl, gm, glast, flat, sided, gf) = rest[:15]
-    (r0, s1, r1a, r1b, s2a, s2b, r2a, r2b, s3a, s3b, r3a, r3b, rt0, re0, st1, rt1, st2, rt2, rt3, g1, g2, g3,
+    (r0, s1, r1a, r1b, s2a, s2b, r2a, r2b, s3a, s3b, r3a, r3b, rt0, re0, st1, rt1, st2, rt2, rt3, g1, g2, g3, rel_a, rel_b,
      send, recv) = rest[15:]
     loads = [pltpu.make_async_copy(sources[i], inputs[i], sems.at[i]) for i in range(12)]
     for i in (9, 11, 10, 0, 2, 1, 8, 3, 4, 5, 6, 7):
@@ -84,9 +84,8 @@
         for copy in group:
             copy.wait_recv()
 
-    for load in loads:
-        load.wait()
-
+    for i in (9, 0, 11, 2, 10, 8):
+        loads[i].wait()
     bf16, f32 = jnp.bfloat16, jnp.float32
     high = lax.Precision.HIGHEST
 
@@ -94,16 +93,17 @@
         return (lax.broadcasted_iota(jnp.int32, (count, row.shape[1]), 0) == row).astype(kind)
 
     hot_one = hot(digit_one[...], 200, bf16)
-    hot_two = hot(digit_two[...], 200, bf16)
+    first[...] = contract(one[...], hot_one, 0, 0)
     hot_three = hot(digit_three[...], 250, bf16)
-    bag = hot(bags[...], 64, f32)
-    first[...] = contract(one[...], hot_one, 0, 0)
     ends = contract(three[...], hot_three, 0, 0)
     last[...] = ends
     for side in range(2):
         sided[side] = ends[:, side * 128:side * 128 + 128]
         for d in range(8):
             turned[d * 32:d * 32 + 32, side * 128:side * 128 + 128] = sided.at[side][pl.ds(d, 32, stride=8), :]
+    hot_two = hot(digit_two[...], 200, bf16)
+    bag = hot(bags[...], 64, f32)
+    loads[1].wait()
     for part in range(8):
         mid[part * 512:part * 512 + 512, :] = contract(two[:, part * 512:part * 512 + 512], hot_two, 0, 0)
 
@@ -122,6 +122,8 @@
         rows.append(total)
     embedded = jnp.concatenate(rows, axis=0)
 
+    for i in (3, 4, 5, 6, 7):
+        loads[i].wait()
     pooled = contract(bag, embedded, 1, 1, precision=high)
     joined = jnp.concatenate([dense[...], pooled.astype(bf16)], axis=1)
     pre = jnp.dot(joined, w_top[...], preferred_element_type=f32) + bias[...]
@@ -161,24 +163,51 @@
         upper, lower = halves(value)
         return contract(table, upper, 1, 1) + contract(table, lower, 1, 1)
 
-    for a in range(0, 32, 2):
-        for half in range(2):
-            c = a + half
-            partial = [jnp.zeros((8, 256), f32) for _ in range(4)]
-            for b in range(16):
-                piece = mid[c * 128 + b * 8:c * 128 + b * 8 + 8, :]
-                total = jnp.zeros((8, 256), f32)
+    def middles(low_a, high_a):
+        for a in range(low_a, high_a, 2):
+            for c in (a, a + 1):
+                partial = [jnp.zeros((8, 256), f32) for _ in range(4)]
+                scale = [jnp.broadcast_to(first[i * 32 + c:i * 32 + c + 1, :], (8, 256)) for i in range(4)]
+                for b in range(8):
+                    totals = []
+                    for at in (c * 128 + b * 16, c * 128 + b * 16 + 8):
+                        piece = mid[at:at + 8, :]
+                        total = None
+                        for i in range(4):
+                            low_at = i * 128 + at - c * 128
+                            slope = gl[low_at:low_at + 8, :]
+                            total = scale[i] * slope if total is None else total + scale[i] * slope
+                            partial[i] = partial[i] + slope * piece
+                        totals.append(total)
+                    gm[c * 128 + b * 16:c * 128 + b * 16 + 16, :] = jnp.concatenate(totals, axis=0).astype(bf16)
                 for i in range(4):
-                    slope = gl[i * 128 + b * 8:i * 128 + b * 8 + 8, :]
-                    total = total + first[i * 32 + c:i * 32 + c + 1, :] * slope
-                    partial[i] = partial[i] + slope * piece
-                gm[half * 128 + b * 8:half * 128 + b * 8 + 8, :] = total
-            for i in range(4):
-                for side in range(2):
-                    gf.at[side][pl.ds(i * 32 + c, 8, stride=128), :] = partial[i][:, side * 128:side * 128 + 128]
-        middle = scatter(hot_two, gm[...])
-        flat[pl.ds(200 + a, 200, stride=32), :] = middle[:, 0:128]
-        flat[pl.ds(201 + a, 200, stride=32), :] = middle[:, 128:256]
+                    for side in range(2):
+                        gf.at[side][pl.ds(i * 32 + c, 8, stride=128), :] = partial[i][:, side * 128:side * 128 + 128]
+            middle = contract(hot_two, gm[a * 128:a * 128 + 256, :], 1, 1)
+            flat[pl.ds(200 + a, 200, stride=32), :] = middle[:, 0:128]
+            flat[pl.ds(201 + a, 200, stride=32), :] = middle[:, 128:256]
+
+    arrived(t0)
+    extra = e[...] + re0[...]
+    for part in range(4):
+        rows = pl.ds(part * 64, 64)
+        st1[part, 0:64, :] = t[core, rows, :] + rt0[rows, :]
+        st1[part, 64:72, :] = extra
+    t1 = [put(st1.at[(x + k) % 4], rt1.at[x], other_x[k]) for k in XORDER]
+    rt1[x] = st1[x]
+
+    middles(0, 16)
+    arrived(t1)
+    total = rt1[0]
+    for part in range(1, 4):
+        total = total + rt1[part]
+    for part in range(8):
+        st2[part, 0:8, :] = total[part * 8:part * 8 + 8]
+        st2[part, 8:16, :] = total[64:72]
+    t2 = [put(st2.at[(v + k) % 8], rt2.at[v], other_v[k]) for k in ORDER]
+    rt2[v] = st2[v]
+
+    middles(16, 32)
     spread = scatter(hot_one, jnp.concatenate([gf[0], gf[1]], axis=1))
     total = spread[:, 0:128]
     for part in range(1, 8):
@@ -193,42 +222,11 @@
         side, qx, qy = (q // 16) % 2, (q // 32) % 4, q % 8
         qz = (q // 128) * 2 + (q // 8) % 2
         qu, qv = (qy, qz) if side == 0 else (qz, qy)
-        start, upper_at, lower_at = (1775 * q) // 128, (qx * 64 + qu * 8 + qv) * 8, (qu * 32 + qv * 4 + qx) * 8
+        start, upper_at, lower_at = (1775 * q) // 128, (qx * 64 + qu * 8 + qv) * 8, (qu * 32 + qx * 8 + qv) * 8
         w[side, 0, upper_at:upper_at + 8, :] = flat[start:start + 8, :]
         w[side, 1, lower_at:lower_at + 8, :] = flat[start + 8:start + 16, :]
 
-    p0 = [put(w.at[1 - core, color], r0.at[color], mate) for color in (0, 1)]
-    arrived(t0)
-    extra = e[...] + re0[...]
-    for part in range(4):
-        rows = pl.ds(part * 64, 64)
-        st1[part, 0:64, :] = t[core, rows, :] + rt0[rows, :]
-        st1[part, 64:72, :] = extra
-    t1 = [put(st1.at[(x + k) % 4], rt1.at[x], other_x[k]) for k in XORDER]
-    rt1[x] = st1[x]
-
-
-    def fold(color):
-        def store(at, value):
-            s1[color, at, :] = value
-        summed(2048, 256, store, lambda at: w[core, color, at, :], lambda at: r0[color, at, :])
-
-    arrived(p0[:1])
-    fold(0)
-    p1a = [put(s1.at[0, pl.ds(((x + k) % 4) * 512, 512)], r1a.at[k - 1], other_x[k]) for k in XORDER]
-    arrived(p0[1:])
-    fold(1)
-    p1b = [put(s1.at[1, pl.ds(((u + k) % 8) * 256, 256)], r1b.at[k - 1], other_u[k]) for k in ORDER]
-
-    arrived(t1)
-    total = rt1[0]
-    for part in range(1, 4):
-        total = total + rt1[part]
-    for part in range(8):
-        st2[part, 0:8, :] = total[part * 8:part * 8 + 8]
-        st2[part, 8:16, :] = total[64:72]
-    t2 = [put(st2.at[(v + k) % 8], rt2.at[v], other_v[k]) for k in ORDER]
-    rt2[v] = st2[v]
+    p0 = [put(w.at[1 - core, color], r0.at[color], mate) for color in (1, 0)]
     arrived(t2)
     total = rt2[0]
     for part in range(1, 8):
@@ -236,22 +234,43 @@
     rt3[u] = total
     t3 = [put(rt3.at[u], rt3.at[u], other_u[k]) for k in ORDER]
 
-    arrived(p1a)
-
-    def store2a(at, value):
-        s2a[at, :] = value
-
-    summed(512, 128, store2a, lambda at: s1[0, pl.ds(x * 512 + at.start, at.size), :],
-           *[functools.partial(lambda k, at: r1a[k, at, :], k) for k in range(3)])
-    p2a = [put(s2a.at[pl.ds(((u + k) % 8) * 64, 64)], r2a.at[k - 1], other_u[k]) for k in ORDER]
-    arrived(p1b)
-
-    def store2b(at, value):
-        s2b[at, :] = value
-
-    summed(256, 64, store2b, lambda at: s1[1, pl.ds(u * 256 + at.start, at.size), :],
-           *[functools.partial(lambda k, at: r1b[k, at, :], k) for k in range(7)])
-    p2b = [put(s2b.at[pl.ds(((v + k) % 8) * 32, 32)], r2b.at[k - 1], other_v[k]) for k in ORDER]
+    def fold(color):
+        def store(at, value):
+            s1[color, at, :] = value
+        summed(2048, 256, store, lambda at: w[core, color, at, :], lambda at: r0[color, at, :])
+
+    def part1(color, slot, rows, half=None):
+        size = rows if half is None else rows // 2
+        return s1.at[color, pl.ds(slot * rows + (0 if half is None else half * size), size)]
+
+    def relayed(color, slot, rows, half, came):
+        at = pl.ds(slot * rows + half * (rows // 2), rows // 2)
+        s1[color, at, :] = s1[color, at, :] + came[...]
+
+    arrived(p0[:1])
+    fold(1)
+    far = (u + 4) % 8
+    relay_b = [put(part1(1, far, 256, 0), rel_b.at[0], other_u[2]), put(part1(1, far, 256, 1), rel_b.at[1], other_u[6])]
+    p1b = [put(part1(1, (u + k) % 8, 256), r1b.at[k - 1], other_u[k]) for k in (3, 5)]
+    p1b += [put(part1(1, (u + 2) % 8, 256, 1), r1b.at[1, pl.ds(128, 128)], other_u[2]),
+            put(part1(1, (u + 6) % 8, 256, 0), r1b.at[5, pl.ds(0, 128)], other_u[6])]
+    p1b += [put(part1(1, (u + k) % 8, 256), r1b.at[k - 1], other_u[k]) for k in (1, 7)]
+    arrived(p0[1:])
+    fold(0)
+    across = (x + 2) % 4
+    relay_a = [put(part1(0, across, 512, 0), rel_a.at[0], other_x[1]), put(part1(0, across, 512, 1), rel_a.at[1], other_x[3])]
+    p1a = [put(part1(0, (x + 1) % 4, 512, 1), r1a.at[0, pl.ds(256, 256)], other_x[1]),
+           put(part1(0, (x + 3) % 4, 512, 0), r1a.at[1, pl.ds(0, 256)], other_x[3])]
+    arrived(relay_b)
+    relayed(1, (u + 2) % 8, 256, 0, rel_b.at[0])
+    relayed(1, (u + 6) % 8, 256, 1, rel_b.at[1])
+    p1b += [put(part1(1, (u + 2) % 8, 256, 0), r1b.at[1, pl.ds(0, 128)], other_u[2]),
+            put(part1(1, (u + 6) % 8, 256, 1), r1b.at[5, pl.ds(128, 128)], other_u[6])]
+    arrived(relay_a)
+    relayed(0, (x + 1) % 4, 512, 0, rel_a.at[0])
+    relayed(0, (x + 3) % 4, 512, 1, rel_a.at[1])
+    p1a += [put(part1(0, (x + 1) % 4, 512, 0), r1a.at[0, pl.ds(0, 256)], other_x[1]),
+            put(part1(0, (x + 3) % 4, 512, 1), r1a.at[1, pl.ds(256, 256)], other_x[3])]
 
     arrived(t3)
     total = rt3[0]
@@ -261,34 +280,48 @@
     extra = total[8:16]
     t4 = [put(g1.at[v], g1.at[v], other_v[k]) for k in ORDER]
 
+    arrived(p1a)
+
+    def store2a(at, value):
+        s2a[at, :] = value
+
+    summed(512, 128, store2a, lambda at: s1[0, pl.ds(x * 512 + at.start, at.size), :],
+           *[functools.partial(lambda k, at: r1a[k, at, :], k) for k in range(2)])
+    p2a = [put(s2a.at[pl.ds(((u + k) % 8) * 64, 64)], r2a.at[k - 1], other_u[k]) for k in ORDER]
+    arrived(t4)
+    g2[x] = g1[...]
+    t5 = [put(g2.at[x], g2.at[x], other_x[k]) for k in XORDER]
+    arrived(p1b)
+
+    def store2b(at, value):
+        s2b[at, :] = value
+
+    summed(256, 64, store2b, lambda at: s1[1, pl.ds(u * 256 + at.start, at.size), :],
+           *[functools.partial(lambda k, at: r1b[k, at, :], k) for k in (0, 1, 2, 4, 5, 6)])
+    p2b = [put(s2b.at[pl.ds(((x + k) % 4) * 64, 64)], r2b.at[k - 1], other_x[k]) for k in XORDER]
+    arrived(p2b)
+    total = s2b[pl.ds(x * 64, 64), :]
+    for part in range(3):
+        total = total + r2b[part]
+    s3b[...] = total
+    p3b = [put(s3b.at[pl.ds(((v + k) % 8) * 8, 8)], r3b.at[k - 1], other_v[k]) for k in ORDER]
     arrived(p2a)
     total = s2a[pl.ds(u * 64, 64), :]
     for part in range(7):
         total = total + r2a[part]
     s3a[...] = total
     p3a = [put(s3a.at[pl.ds(((v + k) % 8) * 8, 8)], r3a.at[k - 1], other_v[k]) for k in ORDER]
-    arrived(p2b)
-    total = s2b[pl.ds(v * 32, 32), :]
+
+    arrived(t5)
+    t6 = put(g2, g3, mate)
+    arrived(p3b)
+    lower = s3b[pl.ds(v * 8, 8), :]
     for part in range(7):
-        total = total + r2b[part]
-    s3b[...] = total
-    p3b = [put(s3b.at[pl.ds(((x + k) % 4) * 8, 8)], r3b.at[k - 1], other_x[k]) for k in XORDER]
-
-    arrived(t4)
-    g2[x] = g1[...]
-    t5 = [put(g2.at[x], g2.at[x], other_x[k]) for k in XORDER]
-    for copy in t5:
-        copy.wait_recv()
-    t6 = put(g2, g3, mate)
-
+        lower = lower + r3b[part]
     arrived(p3a)
     upper = s3a[pl.ds(v * 8, 8), :]
     for part in range(7):
         upper = upper + r3a[part]
-    arrived(p3b)
-    lower = s3b[pl.ds(x * 8, 8), :]
-    for part in range(3):
-        lower = lower + r3b[part]
     gx, gy = lax.axis_index("gx"), lax.axis_index("gy")
     offset = ((gx * 16 + gy) * 1775) % 128
     turned = pltpu.roll(jnp.concatenate([upper, lower], axis=0), (128 - offset) % 128, 1)
@@ -320,21 +353,21 @@
     bf16, f32, i32 = jnp.bfloat16, jnp.float32, jnp.int32
     kinds = [jax.typeof(arg) for arg in args]
     vmem = pl.BlockSpec(memory_space=pltpu.VMEM)
-    wide = [128, 4096, 256, 256, 512, 128, 512, 256, 256]
-    shapes = [(2, 2048), (2, 2048), (3, 512), (7, 256), (512,), (256,), (7, 64), (7, 32), (64,), (32,), (7, 8), (3, 8),
-              (256,), (8,), (4, 72), (4, 72), (8, 16), (8, 16), (8, 16), (8, 8), (4, 8, 8), (4, 8, 8)]
+    wide = [128, 4096, 256, 256, 512, 128, 512, 4096, 256]
+    shapes = [(2, 2048), (2, 2048), (2, 512), (7, 256), (512,), (256,), (7, 64), (3, 64), (64,), (64,), (7, 8), (7, 8),
+              (256,), (8,), (4, 72), (4, 72), (8, 16), (8, 16), (8, 16), (8, 8), (4, 8, 8), (4, 8, 8), (2, 256), (2, 128)]
     scratch = [pltpu.VMEM(kind.shape, kind.dtype) for kind in kinds] + [pltpu.SemaphoreType.DMA((12,))]
     scratch += [pltpu.VMEM(shape + (128,), f32) for shape in ((2, 2, 2048), (2, 256), (8,))]
-    scratch += [pltpu.VMEM((count, 256), f32) for count in wide]
+    scratch += [pltpu.VMEM((count, 256), bf16 if spot == 7 else f32) for spot, count in enumerate(wide)]
     scratch += [pltpu.VMEM(shape + (128,), f32) for shape in [(7104,), (2, 256), (2, 1024)] + shapes]
-    scratch += [pltpu.SemaphoreType.DMA((70,)), pltpu.SemaphoreType.DMA((70,))]
+    scratch += [pltpu.SemaphoreType.DMA((80,)), pltpu.SemaphoreType.DMA((80,))]
     return pl.pallas_call(
         step_kernel,
         out_shape=(jax.ShapeDtypeStruct((16, 128), f32), jax.ShapeDtypeStruct((258, 256), f32)),
         in_specs=[pl.BlockSpec(memory_space=pl.ANY)] * 12,
         out_specs=(vmem, vmem),
         scratch_shapes=scratch,
-        compiler_params=pltpu.CompilerParams(collective_id=0, has_side_effects=True, vmem_limit_bytes=36 * 1024 * 1024),
+        compiler_params=pltpu.CompilerParams(collective_id=0, has_side_effects=True, vmem_limit_bytes=58 * 1024 * 1024),
         name="step",
     )(*args)
 

time: 68.6 us -> 57.6 us (0.84)
  the two profiles are of different devices: /device:TPU:1 before, /device:TPU:2 now
where the time goes in v4:
time: 57.6 us; the launch traced here: 57.4 us
  Pallas kernels  53.8 us (93%)
  local copies, waits for them, and re-layouts  2.97 us (5%)
  between operations  0.64 us (1%)
    pallas_call x1, Pallas kernels, step(): pl.pallas_call(step_kernel, out_shape=(jax.ShapeDtypeStruct((16, 128), f3...  53.8 us
    unnamed x2, local copies, waits for them, and re-layouts  2.97 us

profile of v4, /device:TPU:2, one launch (start us, length us, event | category | flops | bytes accessed | tf_op | source)
XLA Modules:
  0.0 57.4 jit_solution(11785184275178266133)
XLA Ops:
  0.6 53.8 %step.1 = (f32[16,128]{1,0:T(8,128)}, f32[258,256]{1,0:T(8,128)}) custom-call(bf16[200,128]{1,0:T(8,128)(2,1)} %refs_0_.1, bf16[200,4096]{1,0:T(8,128)(2,1)} %refs_1_.1, bf16[250,256]{1,0:T(8,128)(2,1)} %refs_2_.1, bf16[64,128]{1,0:T(8,128)(2,1)} %refs_3_.1, bf16[256,256]{1,0:T(8,128)(2,1)} %refs_4_.1, f32[1,256]{1,0:T(1,128)} %bitcast.6, f32[1,256]{1,0:T(1,128)} %bitcast.7, ...), custom_call_target="tpu_custom_call" | custom-call | tf_op jit(solution)/shard_map/step/pallas_call | solution.py:364
  54.4 1.3 %copy.16 = f32[1775]{0:T(1024)} copy(f32[1775]{0:T(1024)} %bitcast.5) | data formatting | bytes 14200
  55.7 1.7 %copy.17 = f32[258,256]{1,0:T(8,128)} copy(f32[258,256]{1,0:T(8,128)} %get-tuple-element.9) | data formatting | bytes 528384

commit v5 on v4

--- a/solution.py
+++ b/solution.py
@@ -52,9 +52,9 @@
     sources, (out, top), rest = refs[:12], refs[12:14], refs[14:]
     inputs, sems, rest = rest[:12], rest[12], rest[13:]
     one, two, three, dense, w_top, bias, w_out, labels, bags, digit_one, digit_two, digit_three = inputs
-    (w, t, e, first, mid, last, turned, left, g, gl, gm, glast, flat, sided, gf) = rest[:15]
-    (r0, s1, r1a, r1b, s2a, s2b, r2a, r2b, s3a, s3b, r3a, r3b, rt0, re0, st1, rt1, st2, rt2, rt3, g1, g2, g3, rel_a, rel_b,
-     send, recv) = rest[15:]
+    (wa, wb, t, e, first, mid, last, turned, left, g, gl, gm, glast, flat, sided, gf) = rest[:16]
+    (r0a, r0b, s1a, s1b, r1a, r1b, s2a, s2b, r2a, r2b, s3a, s3b, r3a, r3b, rt0, re0, st1, rt1, st2, rt2, rt3, g1, g2, g3, rel_a, rel_b,
+     send, recv) = rest[16:]
     loads = [pltpu.make_async_copy(sources[i], inputs[i], sems.at[i]) for i in range(12)]
     for i in (9, 11, 10, 0, 2, 1, 8, 3, 4, 5, 6, 7):
         loads[i].start()
@@ -179,14 +179,18 @@
                             total = scale[i] * slope if total is None else total + scale[i] * slope
                             partial[i] = partial[i] + slope * piece
                         totals.append(total)
-                    gm[c * 128 + b * 16:c * 128 + b * 16 + 16, :] = jnp.concatenate(totals, axis=0).astype(bf16)
+                    upper, lower = halves(jnp.concatenate(totals, axis=0))
+                    gm[0, c * 128 + b * 16:c * 128 + b * 16 + 16, :] = upper
+                    gm[1, c * 128 + b * 16:c * 128 + b * 16 + 16, :] = lower
                 for i in range(4):
                     for side in range(2):
-                        gf.at[side][pl.ds(i * 32 + c, 8, stride=128), :] = partial[i][:, side * 128:side * 128 + 128]
-            middle = contract(hot_two, gm[a * 128:a * 128 + 256, :], 1, 1)
-            flat[pl.ds(200 + a, 200, stride=32), :] = middle[:, 0:128]
-            flat[pl.ds(201 + a, 200, stride=32), :] = middle[:, 128:256]
-
+                        gf.at[side][pl.ds(i * 32 + c, 8, stride=129), :] = partial[i][:, side * 128:side * 128 + 128]
+            middle = contract(hot_two, gm[0, a * 128:a * 128 + 256, :], 1, 1)
+            middle = middle + contract(hot_two, gm[1, a * 128:a * 128 + 256, :], 1, 1)
+            flat[pl.ds(200 + a, 200, stride=33), :] = middle[:, 0:128]
+            flat[pl.ds(201 + a, 200, stride=33), :] = middle[:, 128:256]
+
+    middles(0, 16)
     arrived(t0)
     extra = e[...] + re0[...]
     for part in range(4):
@@ -196,7 +200,54 @@
     t1 = [put(st1.at[(x + k) % 4], rt1.at[x], other_x[k]) for k in XORDER]
     rt1[x] = st1[x]
 
-    middles(0, 16)
+    ending = scatter(hot_three, glast[...])
+    flat[pl.ds(6800, 250, stride=2), :] = ending[:, 0:128]
+    flat[pl.ds(6801, 250, stride=2), :] = ending[:, 128:256]
+    middles(16, 32)
+    total = jnp.zeros((200, 128), f32)
+    for part in range(0, 8, 2):
+        pieces = [gf[side, at * 129:at * 129 + 128, :] for at in (part, part + 1) for side in (0, 1)]
+        spread = scatter(hot_one, jnp.concatenate([jnp.concatenate(pieces[:2], axis=1), jnp.concatenate(pieces[2:], axis=1)], axis=0))
+        total = total + spread[:, 0:128] + spread[:, 128:256]
+    flat[0:200, :] = total
+    flat[7300:7312, :] = jnp.zeros((12, 128), f32)
+
+    def rows_from(start):
+        spans, at = [], start
+        while at < start + 8:
+            if at < 200:
+                size, place_at = min(200 - at, start + 8 - at), at
+            elif at < 6600:
+                size, place_at = min(32 - (at - 200) % 32, start + 8 - at), 200 + (at - 200) // 32 * 33 + (at - 200) % 32
+            else:
+                size, place_at = start + 8 - at, at + 200
+            spans.append((at - start, size, place_at))
+            at += size
+        return spans
+
+    for q in range(512):
+        side, qx, qy = (q // 16) % 2, (q // 32) % 4, q % 8
+        qz = (q // 128) * 2 + (q // 8) % 2
+        qu, qv = (qy, qz) if side == 0 else (qz, qy)
+        for color, slot in ((0, qx * 64 + qu * 8 + qv), (1, qu * 32 + qx * 8 + qv)):
+            for shift, size, place_at in rows_from((1775 * q) // 128 + 8 * color):
+                if color == 0:
+                    wa[side, slot * 8 + shift:slot * 8 + shift + size, :] = flat[place_at:place_at + size, :]
+                else:
+                    wb[side, slot, shift:shift + size, :] = flat[place_at:place_at + size, :]
+
+    plan = ((0, 2), (1, 4), (1, 3), (1, 5), (0, 1), (0, 3), (1, 2), (1, 6), (1, 1), (1, 7), (0, 0), (1, 0))
+
+    def piece_of(color, distance, x_at, u_at):
+        return pl.ds(((x_at + distance) % 4) * 512, 512) if color == 0 else pl.ds(((u_at + distance) % 8) * 32, 32)
+
+    p0 = {}
+    for color, distance in plan:
+        rows = piece_of(color, distance, x, v)
+        if color == 0:
+            p0[color, distance] = put(wa.at[1 - core, rows], r0a.at[rows], mate)
+        else:
+            p0[color, distance] = put(wb.at[1 - core, rows, pl.ds(0, 7)], r0b.at[rows, pl.ds(0, 7)], mate)
     arrived(t1)
     total = rt1[0]
     for part in range(1, 4):
@@ -207,70 +258,69 @@
     t2 = [put(st2.at[(v + k) % 8], rt2.at[v], other_v[k]) for k in ORDER]
     rt2[v] = st2[v]
 
-    middles(16, 32)
-    spread = scatter(hot_one, jnp.concatenate([gf[0], gf[1]], axis=1))
-    total = spread[:, 0:128]
-    for part in range(1, 8):
-        total = total + spread[:, part * 128:part * 128 + 128]
-    flat[7096:7104, :] = jnp.zeros((8, 128), f32)
-    flat[0:200, :] = total
-    ending = scatter(hot_three, glast[...])
-    flat[pl.ds(6600, 250, stride=2), :] = ending[:, 0:128]
-    flat[pl.ds(6601, 250, stride=2), :] = ending[:, 128:256]
-
-    for q in range(512):
-        side, qx, qy = (q // 16) % 2, (q // 32) % 4, q % 8
-        qz = (q // 128) * 2 + (q // 8) % 2
-        qu, qv = (qy, qz) if side == 0 else (qz, qy)
-        start, upper_at, lower_at = (1775 * q) // 128, (qx * 64 + qu * 8 + qv) * 8, (qu * 32 + qx * 8 + qv) * 8
-        w[side, 0, upper_at:upper_at + 8, :] = flat[start:start + 8, :]
-        w[side, 1, lower_at:lower_at + 8, :] = flat[start + 8:start + 16, :]
-
-    p0 = [put(w.at[1 - core, color], r0.at[color], mate) for color in (1, 0)]
+    def fold(color, distance):
+        p0[color, distance].wait_recv()
+        rows = piece_of(color, distance, x, u)
+        if color == 0:
+            s1a[rows, :] = wa[core, rows, :] + r0a[rows, :]
+        else:
+            s1b[rows, 0:7] = wb[core, rows, 0:7] + r0b[rows, 0:7]
+
+    def part_a(slot, half):
+        return s1a.at[pl.ds(slot * 512 + half * 256, 256)]
+
+    def part_b(slot, start=0, size=32):
+        return s1b.at[pl.ds(slot * 32 + start, size), pl.ds(0, 7)]
+
+    def land_b(k, start=0, size=32):
+        return r1b.at[k - 1, pl.ds(start, size), pl.ds(0, 7)]
+
+    def relayed_a(slot, half, came):
+        at = pl.ds(slot * 512 + half * 256, 256)
+        s1a[at, :] = s1a[at, :] + came[...]
+
+    def relayed_b(slot, half, way):
+        at = pl.ds(slot * 32 + half * 16, 16)
+        s1b[at, 0:7] = s1b[at, 0:7] + rel_b[way, :, 0:7]
+
+    far, across = (u + 4) % 8, (x + 2) % 4
+    fold(0, 2)
+    relay_a = [put(part_a(across, 0), rel_a.at[0], other_x[1]), put(part_a(across, 1), rel_a.at[1], other_x[3])]
+    fold(1, 4)
+    relay_b = [put(part_b(far, 0, 16), rel_b.at[0, :, pl.ds(0, 7)], other_u[2]), put(part_b(far, 16, 16), rel_b.at[1, :, pl.ds(0, 7)], other_u[6])]
+    p1a, p1b = [], []
+    for k in (3, 5):
+        fold(1, k)
+        p1b.append(put(part_b((u + k) % 8), land_b(k), other_u[k]))
+    fold(0, 1)
+    p1a.append(put(part_a((x + 1) % 4, 1), r1a.at[0, pl.ds(256, 256)], other_x[1]))
+    fold(0, 3)
+    p1a.append(put(part_a((x + 3) % 4, 0), r1a.at[1, pl.ds(0, 256)], other_x[3]))
+    fold(1, 2)
+    p1b.append(put(part_b((u + 2) % 8, 16, 16), land_b(2, 16, 16), other_u[2]))
+    fold(1, 6)
+    p1b.append(put(part_b((u + 6) % 8, 0, 16), land_b(6, 0, 16), other_u[6]))
     arrived(t2)
     total = rt2[0]
     for part in range(1, 8):
         total = total + rt2[part]
     rt3[u] = total
     t3 = [put(rt3.at[u], rt3.at[u], other_u[k]) for k in ORDER]
-
-    def fold(color):
-        def store(at, value):
-            s1[color, at, :] = value
-        summed(2048, 256, store, lambda at: w[core, color, at, :], lambda at: r0[color, at, :])
-
-    def part1(color, slot, rows, half=None):
-        size = rows if half is None else rows // 2
-        return s1.at[color, pl.ds(slot * rows + (0 if half is None else half * size), size)]
-
-    def relayed(color, slot, rows, half, came):
-        at = pl.ds(slot * rows + half * (rows // 2), rows // 2)
-        s1[color, at, :] = s1[color, at, :] + came[...]
-
-    arrived(p0[:1])
-    fold(1)
-    far = (u + 4) % 8
-    relay_b = [put(part1(1, far, 256, 0), rel_b.at[0], other_u[2]), put(part1(1, far, 256, 1), rel_b.at[1], other_u[6])]
-    p1b = [put(part1(1, (u + k) % 8, 256), r1b.at[k - 1], other_u[k]) for k in (3, 5)]
-    p1b += [put(part1(1, (u + 2) % 8, 256, 1), r1b.at[1, pl.ds(128, 128)], other_u[2]),
-            put(part1(1, (u + 6) % 8, 256, 0), r1b.at[5, pl.ds(0, 128)], other_u[6])]
-    p1b += [put(part1(1, (u + k) % 8, 256), r1b.at[k - 1], other_u[k]) for k in (1, 7)]
-    arrived(p0[1:])
-    fold(0)
-    across = (x + 2) % 4
-    relay_a = [put(part1(0, across, 512, 0), rel_a.at[0], other_x[1]), put(part1(0, across, 512, 1), rel_a.at[1], other_x[3])]
-    p1a = [put(part1(0, (x + 1) % 4, 512, 1), r1a.at[0, pl.ds(256, 256)], other_x[1]),
-           put(part1(0, (x + 3) % 4, 512, 0), r1a.at[1, pl.ds(0, 256)], other_x[3])]
+    for k in (1, 7):
+        fold(1, k)
+        p1b.append(put(part_b((u + k) % 8), land_b(k), other_u[k]))
+    fold(0, 0)
+    fold(1, 0)
     arrived(relay_b)
-    relayed(1, (u + 2) % 8, 256, 0, rel_b.at[0])
-    relayed(1, (u + 6) % 8, 256, 1, rel_b.at[1])
-    p1b += [put(part1(1, (u + 2) % 8, 256, 0), r1b.at[1, pl.ds(0, 128)], other_u[2]),
-            put(part1(1, (u + 6) % 8, 256, 1), r1b.at[5, pl.ds(128, 128)], other_u[6])]
+    relayed_b((u + 2) % 8, 0, 0)
+    relayed_b((u + 6) % 8, 1, 1)
+    p1b += [put(part_b((u + 2) % 8, 0, 16), land_b(2, 0, 16), other_u[2]),
+            put(part_b((u + 6) % 8, 16, 16), land_b(6, 16, 16), other_u[6])]
     arrived(relay_a)
-    relayed(0, (x + 1) % 4, 512, 0, rel_a.at[0])
-    relayed(0, (x + 3) % 4, 512, 1, rel_a.at[1])
-    p1a += [put(part1(0, (x + 1) % 4, 512, 0), r1a.at[0, pl.ds(0, 256)], other_x[1]),
-            put(part1(0, (x + 3) % 4, 512, 1), r1a.at[1, pl.ds(256, 256)], other_x[3])]
+    relayed_a((x + 1) % 4, 0, rel_a.at[0])
+    relayed_a((x + 3) % 4, 1, rel_a.at[1])
+    p1a += [put(part_a((x + 1) % 4, 0), r1a.at[0, pl.ds(0, 256)], other_x[1]),
+            put(part_a((x + 3) % 4, 1), r1a.at[1, pl.ds(256, 256)], other_x[3])]
 
     arrived(t3)
     total = rt3[0]
@@ -285,26 +335,30 @@
     def store2a(at, value):
         s2a[at, :] = value
 
-    summed(512, 128, store2a, lambda at: s1[0, pl.ds(x * 512 + at.start, at.size), :],
+    summed(512, 128, store2a, lambda at: s1a[pl.ds(x * 512 + at.start, at.size), :],
            *[functools.partial(lambda k, at: r1a[k, at, :], k) for k in range(2)])
     p2a = [put(s2a.at[pl.ds(((u + k) % 8) * 64, 64)], r2a.at[k - 1], other_u[k]) for k in ORDER]
+    arrived(p1b)
+
+    def fold2(part, carry):
+        at = pl.ds(pl.multiple_of(part * 8, 8), 8)
+        total = s1b[pl.ds(u * 32 + part * 8, 8), 0:7]
+        for k in (1, 2, 3, 5, 6, 7):
+            total = total + r1b[k - 1, at, 0:7]
+        s2b[at, 0:7] = total
+        return carry
+
+    lax.fori_loop(0, 4, fold2, 0)
+    p2b = [put(s2b.at[pl.ds(((x + k) % 4) * 8, 8), pl.ds(0, 7)], r2b.at[k - 1, :, pl.ds(0, 7)], other_x[k]) for k in XORDER]
+    arrived(p2b)
+    total = s2b[pl.ds(x * 8, 8), 0:7]
+    for part in range(3):
+        total = total + r2b[part, :, 0:7]
+    s3b[:, 0:7] = total
+    p3b = [put(s3b.at[(v + k) % 8, pl.ds(0, 7)], r3b.at[k - 1, pl.ds(0, 7)], other_v[k]) for k in ORDER]
     arrived(t4)
     g2[x] = g1[...]
     t5 = [put(g2.at[x], g2.at[x], other_x[k]) for k in XORDER]
-    arrived(p1b)
-
-    def store2b(at, value):
-        s2b[at, :] = value
-
-    summed(256, 64, store2b, lambda at: s1[1, pl.ds(u * 256 + at.start, at.size), :],
-           *[functools.partial(lambda k, at: r1b[k, at, :], k) for k in (0, 1, 2, 4, 5, 6)])
-    p2b = [put(s2b.at[pl.ds(((x + k) % 4) * 64, 64)], r2b.at[k - 1], other_x[k]) for k in XORDER]
-    arrived(p2b)
-    total = s2b[pl.ds(x * 64, 64), :]
-    for part in range(3):
-        total = total + r2b[part]
-    s3b[...] = total
-    p3b = [put(s3b.at[pl.ds(((v + k) % 8) * 8, 8)], r3b.at[k - 1], other_v[k]) for k in ORDER]
     arrived(p2a)
     total = s2a[pl.ds(u * 64, 64), :]
     for part in range(7):
@@ -315,9 +369,10 @@
     arrived(t5)
     t6 = put(g2, g3, mate)
     arrived(p3b)
-    lower = s3b[pl.ds(v * 8, 8), :]
+    lower = s3b[v, 0:7]
     for part in range(7):
-        lower = lower + r3b[part]
+        lower = lower + r3b[part, 0:7]
+    lower = jnp.concatenate([lower, jnp.zeros((1, 128), f32)], axis=0)
     arrived(p3a)
     upper = s3a[pl.ds(v * 8, 8), :]
     for part in range(7):
@@ -353,14 +408,15 @@
     bf16, f32, i32 = jnp.bfloat16, jnp.float32, jnp.int32
     kinds = [jax.typeof(arg) for arg in args]
     vmem = pl.BlockSpec(memory_space=pltpu.VMEM)
-    wide = [128, 4096, 256, 256, 512, 128, 512, 4096, 256]
-    shapes = [(2, 2048), (2, 2048), (2, 512), (7, 256), (512,), (256,), (7, 64), (3, 64), (64,), (64,), (7, 8), (7, 8),
-              (256,), (8,), (4, 72), (4, 72), (8, 16), (8, 16), (8, 16), (8, 8), (4, 8, 8), (4, 8, 8), (2, 256), (2, 128)]
+    wide = [128, 4096, 256, 256, 512, 128, 512, None, 256]
+    shapes = [(2048,), (256, 8), (2048,), (256, 8), (2, 512), (7, 32, 8), (512,), (32, 8), (7, 64), (3, 8, 8), (64,), (8, 8),
+              (7, 8), (7, 8),
+              (256,), (8,), (4, 72), (4, 72), (8, 16), (8, 16), (8, 16), (8, 8), (4, 8, 8), (4, 8, 8), (2, 256), (2, 16, 8)]
     scratch = [pltpu.VMEM(kind.shape, kind.dtype) for kind in kinds] + [pltpu.SemaphoreType.DMA((12,))]
-    scratch += [pltpu.VMEM(shape + (128,), f32) for shape in ((2, 2, 2048), (2, 256), (8,))]
-    scratch += [pltpu.VMEM((count, 256), bf16 if spot == 7 else f32) for spot, count in enumerate(wide)]
-    scratch += [pltpu.VMEM(shape + (128,), f32) for shape in [(7104,), (2, 256), (2, 1024)] + shapes]
-    scratch += [pltpu.SemaphoreType.DMA((80,)), pltpu.SemaphoreType.DMA((80,))]
+    scratch += [pltpu.VMEM(shape + (128,), f32) for shape in ((2, 2048), (2, 256, 8), (2, 256), (8,))]
+    scratch += [pltpu.VMEM((count, 256), f32) if count else pltpu.VMEM((2, 4096, 256), bf16) for count in wide]
+    scratch += [pltpu.VMEM(shape + (128,), f32) for shape in [(7312,), (2, 256), (2, 1032)] + shapes]
+    scratch += [pltpu.SemaphoreType.DMA((90,)), pltpu.SemaphoreType.DMA((90,))]
     return pl.pallas_call(
         step_kernel,
         out_shape=(jax.ShapeDtypeStruct((16, 128), f32), jax.ShapeDtypeStruct((258, 256), f32)),

time: 57.6 us -> 52.3 us (0.908)
  the two profiles are of different devices: /device:TPU:2 before, /device:TPU:1 now
where the time goes in v5:
time: 52.3 us; the launch traced here: 52.1 us
  Pallas kernels  48.5 us (93%)
  local copies, waits for them, and re-layouts  2.97 us (6%)
  between operations  0.64 us (1%)
    pallas_call x1, Pallas kernels, step(): pl.pallas_call(step_kernel, out_shape=(jax.ShapeDtypeStruct((16, 128), f3...  48.5 us
    unnamed x2, local copies, waits for them, and re-layouts  2.97 us

profile of v5, /device:TPU:1, one launch (start us, length us, event | category | flops | bytes accessed | tf_op | source)
XLA Modules:
  0.0 52.1 jit_solution(12233097709807987868)
XLA Ops:
  0.6 48.5 %step.1 = (f32[16,128]{1,0:T(8,128)}, f32[258,256]{1,0:T(8,128)}) custom-call(bf16[200,128]{1,0:T(8,128)(2,1)} %refs_0_.1, bf16[200,4096]{1,0:T(8,128)(2,1)} %refs_1_.1, bf16[250,256]{1,0:T(8,128)(2,1)} %refs_2_.1, bf16[64,128]{1,0:T(8,128)(2,1)} %refs_3_.1, bf16[256,256]{1,0:T(8,128)(2,1)} %refs_4_.1, f32[1,256]{1,0:T(1,128)} %bitcast.6, f32[1,256]{1,0:T(1,128)} %bitcast.7, ...), custom_call_target="tpu_custom_call" | custom-call | tf_op jit(solution)/shard_map/step/pallas_call | solution.py:420
  49.1 1.3 %copy.16 = f32[1775]{0:T(1024)} copy(f32[1775]{0:T(1024)} %bitcast.5) | data formatting | bytes 14200
  50.4 1.7 %copy.17 = f32[258,256]{1,0:T(8,128)} copy(f32[258,256]{1,0:T(8,128)} %get-tuple-element.9) | data formatting | bytes 528384

commit v6 on v5

--- a/solution.py
+++ b/solution.py
@@ -350,15 +350,15 @@
 
     lax.fori_loop(0, 4, fold2, 0)
     p2b = [put(s2b.at[pl.ds(((x + k) % 4) * 8, 8), pl.ds(0, 7)], r2b.at[k - 1, :, pl.ds(0, 7)], other_x[k]) for k in XORDER]
+    arrived(t4)
+    g2[x] = g1[...]
+    t5 = [put(g2.at[x], g2.at[x], other_x[k]) for k in XORDER]
     arrived(p2b)
     total = s2b[pl.ds(x * 8, 8), 0:7]
     for part in range(3):
         total = total + r2b[part, :, 0:7]
     s3b[:, 0:7] = total
     p3b = [put(s3b.at[(v + k) % 8, pl.ds(0, 7)], r3b.at[k - 1, pl.ds(0, 7)], other_v[k]) for k in ORDER]
-    arrived(t4)
-    g2[x] = g1[...]
-    t5 = [put(g2.at[x], g2.at[x], other_x[k]) for k in XORDER]
     arrived(p2a)
     total = s2a[pl.ds(u * 64, 64), :]
     for part in range(7):
@@ -420,12 +420,12 @@
     return pl.pallas_call(
         step_kernel,
         out_shape=(jax.ShapeDtypeStruct((16, 128), f32), jax.ShapeDtypeStruct((258, 256), f32)),
-        in_specs=[pl.BlockSpec(memory_space=pl.ANY)] * 12,
+        in_specs=[pl.BlockSpec(memory_space=pltpu.HBM)] * 12,
         out_specs=(vmem, vmem),
         scratch_shapes=scratch,
-        compiler_params=pltpu.CompilerParams(collective_id=0, has_side_effects=True, vmem_limit_bytes=58 * 1024 * 1024),
+        compiler_params=pltpu.CompilerParams(collective_id=0, has_side_effects=True, vmem_limit_bytes=40 * 1024 * 1024),
         name="step",
-    )(*args)
+    )(*[pltpu.with_memory_space_constraint(arg, pltpu.HBM) for arg in args])
 
 
 def per_device(core_one, core_two, core_three, dense_rows, w_top, bias_top, w_out, labels, bag_ids, digit_one, digit_two,

time: 52.3 us -> 49.6 us (0.948)
  local copies, waits for them, and re-layouts: 2.97 us -> 1.31 us
  Pallas kernels: 48.5 us -> 47.5 us
    unnamed x2, local copies, waits for them, and re-layouts: 2.97 us -> 1.31 us
    pallas_call x1, Pallas kernels: 48.5 us -> 47.5 us  [step(): pl.pallas_call(step_kernel, out_shape=(jax.ShapeDtypeStruct((16, 128), f3...]
where the time goes in v6:
time: 49.6 us; the launch traced here: 49.5 us
  Pallas kernels  47.5 us (96%)
  local copies, waits for them, and re-layouts  1.31 us (3%)
  between operations  0.64 us (1%)
    pallas_call x1, Pallas kernels, step(): pl.pallas_call(step_kernel, out_shape=(jax.ShapeDtypeStruct((16, 128), f3...  47.5 us
    unnamed x2, local copies, waits for them, and re-layouts  1.31 us

profile of v6, /device:TPU:1, one launch (start us, length us, event | category | flops | bytes accessed | tf_op | source)
XLA Modules:
  0.0 49.5 jit_solution(7845362302384501356)
XLA Ops:
  0.6 47.5 %step.1 = (f32[16,128]{1,0:T(8,128)S(1)}, f32[258,256]{1,0:T(8,128)S(1)}) custom-call(bf16[200,128]{1,0:T(8,128)(2,1)} %refs_0_.1, bf16[200,4096]{1,0:T(8,128)(2,1)} %refs_1_.1, bf16[250,256]{1,0:T(8,128)(2,1)} %refs_2_.1, bf16[64,128]{1,0:T(8,128)(2,1)} %refs_3_.1, bf16[256,256]{1,0:T(8,128)(2,1)} %refs_4_.1, f32[1,256]{1,0:T(1,128)} %bitcast.6, ...), custom_call_target="tpu_custom_call" | custom-call | tf_op jit(solution)/shard_map/step/pallas_call | solution.py:420
  48.2 0.6 %copy.16 = f32[1775]{0:T(1024)} copy(f32[1775]{0:T(1024)S(1)} %bitcast.5) | data formatting | bytes 14200
  48.8 0.7 %copy.17 = f32[258,256]{1,0:T(8,128)} copy(f32[258,256]{1,0:T(8,128)S(1)} %get-tuple-element.9) | data formatting | bytes 528384

commit v7 on v6

--- a/solution.py
+++ b/solution.py
@@ -87,7 +87,6 @@
     for i in (9, 0, 11, 2, 10, 8):
         loads[i].wait()
     bf16, f32 = jnp.bfloat16, jnp.float32
-    high = lax.Precision.HIGHEST
 
     def hot(row, count, kind):
         return (lax.broadcasted_iota(jnp.int32, (count, row.shape[1]), 0) == row).astype(kind)
@@ -102,7 +101,7 @@
         for d in range(8):
             turned[d * 32:d * 32 + 32, side * 128:side * 128 + 128] = sided.at[side][pl.ds(d, 32, stride=8), :]
     hot_two = hot(digit_two[...], 200, bf16)
-    bag = hot(bags[...], 64, f32)
+    bag = hot(bags[...], 64, bf16)
     loads[1].wait()
     for part in range(8):
         mid[part * 512:part * 512 + 512, :] = contract(two[:, part * 512:part * 512 + 512], hot_two, 0, 0)
@@ -124,7 +123,8 @@
 
     for i in (3, 4, 5, 6, 7):
         loads[i].wait()
-    pooled = contract(bag, embedded, 1, 1, precision=high)
+    upper, lower = halves(embedded)
+    pooled = contract(bag, upper, 1, 1) + contract(bag, lower, 1, 1)
     joined = jnp.concatenate([dense[...], pooled.astype(bf16)], axis=1)
     pre = jnp.dot(joined, w_top[...], preferred_element_type=f32) + bias[...]
     sig = jax.nn.sigmoid(pre)
@@ -143,7 +143,8 @@
     e[...] = jnp.concatenate([grad_bias[:, :128], grad_bias[:, 128:], grad_out[:, :128], grad_out[:, 128:],
                               jnp.zeros((4, 128), f32)], axis=0)
     pooled_grad = contract(w_top[128:256, :], low, 1, 1)
-    g[...] = jnp.dot(pooled_grad, bag, precision=high, preferred_element_type=f32)
+    upper, lower = halves(pooled_grad)
+    g[...] = contract(upper, bag, 1, 0) + contract(lower, bag, 1, 0)
 
     pl.semaphore_wait(barrier, len(peers))
     t0 = [put(t.at[1 - core], rt0, mate), put(e, re0, mate)]
@@ -225,11 +226,12 @@
             at += size
         return spans
 
-    for q in range(512):
-        side, qx, qy = (q // 16) % 2, (q // 32) % 4, q % 8
-        qz = (q // 128) * 2 + (q // 8) % 2
-        qu, qv = (qy, qz) if side == 0 else (qz, qy)
-        for color, slot in ((0, qx * 64 + qu * 8 + qv), (1, qu * 32 + qx * 8 + qv)):
+    def packed(color):
+        for q in range(512):
+            side, qx, qy = (q // 16) % 2, (q // 32) % 4, q % 8
+            qz = (q // 128) * 2 + (q // 8) % 2
+            qu, qv = (qy, qz) if side == 0 else (qz, qy)
+            slot = qx * 64 + qu * 8 + qv if color == 0 else qu * 32 + qx * 8 + qv
             for shift, size, place_at in rows_from((1775 * q) // 128 + 8 * color):
                 if color == 0:
                     wa[side, slot * 8 + shift:slot * 8 + shift + size, :] = flat[place_at:place_at + size, :]
@@ -242,12 +244,18 @@
         return pl.ds(((x_at + distance) % 4) * 512, 512) if color == 0 else pl.ds(((u_at + distance) % 8) * 32, 32)
 
     p0 = {}
-    for color, distance in plan:
-        rows = piece_of(color, distance, x, v)
-        if color == 0:
-            p0[color, distance] = put(wa.at[1 - core, rows], r0a.at[rows], mate)
-        else:
-            p0[color, distance] = put(wb.at[1 - core, rows, pl.ds(0, 7)], r0b.at[rows, pl.ds(0, 7)], mate)
+    def pair_copies(wanted):
+        for color, distance in wanted:
+            rows = piece_of(color, distance, x, v)
+            if color == 0:
+                p0[color, distance] = put(wa.at[1 - core, rows], r0a.at[rows], mate)
+            else:
+                p0[color, distance] = put(wb.at[1 - core, rows, pl.ds(0, 7)], r0b.at[rows, pl.ds(0, 7)], mate)
+
+    packed(0)
+    pair_copies(plan[:1])
+    packed(1)
+    pair_copies(plan[1:])
     arrived(t1)
     total = rt1[0]
     for part in range(1, 4):
@@ -322,6 +330,14 @@
     p1a += [put(part_a((x + 1) % 4, 0), r1a.at[0, pl.ds(0, 256)], other_x[1]),
             put(part_a((x + 3) % 4, 1), r1a.at[1, pl.ds(256, 256)], other_x[3])]
 
+    arrived(p1a)
+
+    def store2a(at, value):
+        s2a[at, :] = value
+
+    summed(512, 128, store2a, lambda at: s1a[pl.ds(x * 512 + at.start, at.size), :],
+           *[functools.partial(lambda k, at: r1a[k, at, :], k) for k in range(2)])
+    p2a = [put(s2a.at[pl.ds(((u + k) % 8) * 64, 64)], r2a.at[k - 1], other_u[k]) for k in ORDER]
     arrived(t3)
     total = rt3[0]
     for part in range(1, 8):
@@ -329,15 +345,6 @@
     g1[v] = total[0:8]
     extra = total[8:16]
     t4 = [put(g1.at[v], g1.at[v], other_v[k]) for k in ORDER]
-
-    arrived(p1a)
-
-    def store2a(at, value):
-        s2a[at, :] = value
-
-    summed(512, 128, store2a, lambda at: s1a[pl.ds(x * 512 + at.start, at.size), :],
-           *[functools.partial(lambda k, at: r1a[k, at, :], k) for k in range(2)])
-    p2a = [put(s2a.at[pl.ds(((u + k) % 8) * 64, 64)], r2a.at[k - 1], other_u[k]) for k in ORDER]
     arrived(p1b)
 
     def fold2(part, carry):

time: 49.6 us -> 49.5 us (level); the launches traced: 49.5 us -> 48.6 us
  Pallas kernels: 47.5 us -> 46.7 us
    pallas_call x1, Pallas kernels: 47.5 us -> 46.7 us  [step(): pl.pallas_call(step_kernel, out_shape=(jax.ShapeDtypeStruct((16, 128), f3...]
where the time goes in v7:
time: 49.5 us; the launch traced here: 48.6 us
  Pallas kernels  46.7 us (94%)
  local copies, waits for them, and re-layouts  1.31 us (3%)
  between operations  0.64 us (1%)
    pallas_call x1, Pallas kernels, step(): pl.pallas_call(step_kernel, out_shape=(jax.ShapeDtypeStruct((16, 128), f3...  46.7 us
    unnamed x2, local copies, waits for them, and re-layouts  1.31 us

profile of v7, /device:TPU:1, one launch (start us, length us, event | category | flops | bytes accessed | tf_op | source)
XLA Modules:
  0.0 48.6 jit_solution(5958724737594047210)
XLA Ops:
  0.6 46.7 %step.1 = (f32[16,128]{1,0:T(8,128)S(1)}, f32[258,256]{1,0:T(8,128)S(1)}) custom-call(bf16[200,128]{1,0:T(8,128)(2,1)} %refs_0_.1, bf16[200,4096]{1,0:T(8,128)(2,1)} %refs_1_.1, bf16[250,256]{1,0:T(8,128)(2,1)} %refs_2_.1, bf16[64,128]{1,0:T(8,128)(2,1)} %refs_3_.1, bf16[256,256]{1,0:T(8,128)(2,1)} %refs_4_.1, f32[1,256]{1,0:T(1,128)} %bitcast.6, ...), custom_call_target="tpu_custom_call" | custom-call | tf_op jit(solution)/shard_map/step/pallas_call | solution.py:427
  47.3 0.6 %copy.16 = f32[1775]{0:T(1024)} copy(f32[1775]{0:T(1024)S(1)} %bitcast.5) | data formatting | bytes 14200
  47.9 0.7 %copy.17 = f32[258,256]{1,0:T(8,128)} copy(f32[258,256]{1,0:T(8,128)S(1)} %get-tuple-element.9) | data formatting | bytes 528384
